TPU v7x, 32 devices: a whole 2x2x4 slice. The times are simulated.
32 devices in a mesh: fields: 2 (over x), col: 4 (over z), row: 4 (over y, core).
Axes of the slice: x: 2, y: 2, z: 4, core: 2. Of those that a mesh axis runs over, the one named last changes fastest.
Arguments:
- field_u: bfloat16 [64, 128, 128, 128], P('fields', None, 'row', 'col'), parts along dimension 0
- fac_a: bfloat16 [256, 128], P('fields'), parts along dimension 0
- fac_b: bfloat16 [256, 128], P('fields'), parts along dimension 0
- fac_c: bfloat16 [256, 128], P('fields'), parts along dimension 0
- diag_d: float32 [256, 128, 128], P(('fields', 'row'), 'col'), parts along dimension 0
Outputs:
- output: float32 [64, 128, 128, 128], P('fields', None, 'row', 'col'), parts along dimension 0
There are 2 independent parts. A program takes and returns all parts, laid end to end along the dimension named above; each array names one.
All inputs are finite; a program needn't handle non-finite values.
Results may differ from a plain program's by a relative error of at most 0.001.
Values are sent between devices in bfloat16 or wider.
A program may use at most 1 GiB of HBM per device.

v0:
```python
import jax
import jax.numpy as jnp
from jax import lax
from jax.sharding import PartitionSpec as P


def solution(mesh):
    spec_field = P("fields", None, "row", "col")
    spec_factor = P("fields", None)
    spec_diag = P(("fields", "row"), "col", None)

    def local_apply(field_u, fac_a, fac_b, fac_c, diag_d):
        stage_one = jnp.einsum("ix,bxyz->biyz", fac_a, field_u, preferred_element_type=jnp.float32).astype(jnp.bfloat16)
        y_pencil = lax.all_to_all(stage_one, "row", 1, 2, tiled=True)
        stage_two = jnp.einsum("jy,biyz->bijz", fac_b, y_pencil, preferred_element_type=jnp.float32).astype(jnp.bfloat16)
        z_pencil = lax.all_to_all(stage_two, "col", 2, 3, tiled=True)
        stage_three = (jnp.einsum("kz,bijz->bijk", fac_c, z_pencil, preferred_element_type=jnp.float32) * diag_d).astype(jnp.bfloat16)
        stage_four = jnp.einsum("kz,bijk->bijz", fac_c, stage_three, preferred_element_type=jnp.float32).astype(jnp.bfloat16)
        back_y = lax.all_to_all(stage_four, "col", 3, 2, tiled=True)
        stage_five = jnp.einsum("jy,bijz->biyz", fac_b, back_y, preferred_element_type=jnp.float32).astype(jnp.bfloat16)
        back_x = lax.all_to_all(stage_five, "row", 2, 1, tiled=True)
        return jnp.einsum("ix,biyz->bxyz", fac_a, back_x, preferred_element_type=jnp.float32)

    return jax.shard_map(local_apply, mesh=mesh, in_specs=(spec_field, spec_factor, spec_factor, spec_factor, spec_diag), out_specs=spec_field, check_vma=False)
```

profile of v0, /device:TPU:0, one launch (start us, length us, event | category | flops | bytes accessed | tf_op | source)
XLA Modules:
  0.0 1498.7 jit_solution(12794607646634696975)
XLA Ops:
  0.0 0.0 copy-start
  0.0 9.1 convert_bitcast_fusion.2
  9.1 44.2 %copy.13 = bf16[32,128,32,32]{3,2,0,1:T(8,128)(2,1)} copy(bf16[32,128,32,32]{1,3,2,0:T(8,128)(2,1)} %convert_bitcast_fusion.2) | data formatting | bytes 16777216 | tf_op jit(solution)/shard_map/convert_element_type | solution.py:13
  53.3 50.1 %reshape.4 = bf16[4,2,524288]{2,1,0:T(2,128)(2,1)} reshape(bf16[128,32,32,32]{3,2,1,0:T(8,128)(2,1)} %bitcast.59) | data formatting | bytes 16777216
  103.4 101.1 %all_to_all.72 = bf16[4,2,524288]{2,1,0:T(2,128)(2,1)} all-to-all(bf16[4,2,524288]{2,1,0:T(2,128)(2,1)} %reshape.4), channel_id=1, replica_groups=mesh['fields'=2,'col'=4,'row'=4] {'row'}, dimensions={0} | all-to-all | bytes 16777216 | tf_op jit(solution)/shard_map/all_to_all | solution.py:14
  204.6 36.9 %reshape.5 = bf16[128,32,32,32]{3,2,1,0:T(8,128)(2,1)} reshape(bf16[4,2,524288]{2,1,0:T(2,128)(2,1)} %all_to_all.72) | data formatting | bytes 16777216
  241.5 51.1 %copy.14 = bf16[32,4,32,32,32]{3,1,4,2,0:T(4,128)(2,1)} copy(bf16[32,4,32,32,32]{4,3,0,2,1:T(8,128)(2,1)} %bitcast.63) | data formatting | bytes 16777216 | tf_op jit(solution)/shard_map/all_to_all | solution.py:14
  292.5 38.8 %all_to_all.55 = bf16[32,32,128,32]{2,3,1,0:T(8,128)(2,1)} reshape(bf16[32,32,4,32,32]{3,2,4,1,0:T(4,128)(2,1)} %bitcast.64) | data formatting | bytes 16777216 | tf_op jit(solution)/shard_map/all_to_all | solution.py:14
  331.3 0.0 copy-done
  331.3 8.9 convert_bitcast_fusion.1
  340.3 44.2 %copy.15 = bf16[32,32,128,32]{3,1,0,2:T(8,128)(2,1)} copy(bf16[32,32,128,32]{2,3,1,0:T(8,128)(2,1)} %convert_bitcast_fusion.1) | data formatting | bytes 16777216 | tf_op jit(solution)/shard_map/convert_element_type | solution.py:15
  384.4 50.3 %reshape.6 = bf16[4,2,524288]{2,1,0:T(2,128)(2,1)} reshape(bf16[128,32,32,32]{3,2,1,0:T(8,128)(2,1)} %bitcast.60) | data formatting | bytes 16777216
  434.8 191.2 %all_to_all.73 = bf16[4,2,524288]{2,1,0:T(2,128)(2,1)} all-to-all(bf16[4,2,524288]{2,1,0:T(2,128)(2,1)} %reshape.6), channel_id=1, replica_groups=mesh['fields'=2,'col'=4,'row'=4] {'col'}, dimensions={0} | all-to-all | bytes 16777216 | tf_op jit(solution)/shard_map/all_to_all | solution.py:16
  625.9 36.9 %reshape.7 = bf16[128,32,32,32]{3,2,1,0:T(8,128)(2,1)} reshape(bf16[4,2,524288]{2,1,0:T(2,128)(2,1)} %all_to_all.73) | data formatting | bytes 16777216
  662.8 42.1 %copy.27 = bf16[32,32,4,32,32]{4,2,3,1,0:T(4,128)(2,1)} copy(bf16[32,32,4,32,32]{4,1,0,3,2:T(8,128)(2,1)} %bitcast.65) | data formatting | bytes 16777216 | tf_op jit(solution)/shard_map/all_to_all | solution.py:16
  704.9 0.0 copy-start.1
  704.9 0.0 copy-start.2
  704.9 38.9 %all_to_all.59 = bf16[32,32,32,128]{3,2,1,0:T(8,128)(2,1)} reshape(bf16[32,32,32,4,32]{4,3,2,1,0:T(4,128)(2,1)} %bitcast.66) | data formatting | bytes 16777216 | tf_op jit(solution)/shard_map/all_to_all | solution.py:16
  743.8 0.0 copy-done.1
  743.8 0.0 copy-done.2
  743.8 9.2 convolution_convert_fusion
  752.9 44.2 %copy.17 = bf16[32,32,32,128]{2,1,0,3:T(8,128)(2,1)} copy(bf16[32,32,32,128]{3,2,1,0:T(8,128)(2,1)} %convolution_convert_fusion) | data formatting | bytes 16777216 | tf_op jit(solution)/shard_map/convert_element_type | solution.py:18
  797.1 50.6 %reshape.8 = bf16[4,2,524288]{2,1,0:T(2,128)(2,1)} reshape(bf16[128,32,32,32]{3,2,1,0:T(8,128)(2,1)} %bitcast.61) | data formatting | bytes 16777216
  847.7 190.2 %all_to_all.74 = bf16[4,2,524288]{2,1,0:T(2,128)(2,1)} all-to-all(bf16[4,2,524288]{2,1,0:T(2,128)(2,1)} %reshape.8), channel_id=1, replica_groups=mesh['fields'=2,'col'=4,'row'=4] {'col'}, dimensions={0} | all-to-all | bytes 16777216 | tf_op jit(solution)/shard_map/all_to_all | solution.py:19
  1037.9 36.9 %reshape.9 = bf16[128,32,32,32]{3,2,1,0:T(8,128)(2,1)} reshape(bf16[4,2,524288]{2,1,0:T(2,128)(2,1)} %all_to_all.74) | data formatting | bytes 16777216
  1074.8 42.1 %copy.26 = bf16[32,32,32,4,32]{2,3,4,1,0:T(4,128)(2,1)} copy(bf16[32,32,32,4,32]{2,1,0,4,3:T(8,128)(2,1)} %bitcast.67) | data formatting | bytes 16777216 | tf_op jit(solution)/shard_map/all_to_all | solution.py:19
  1116.9 38.8 %all_to_all.63 = bf16[32,32,128,32]{2,3,1,0:T(8,128)(2,1)} reshape(bf16[32,32,4,32,32]{3,2,4,1,0:T(4,128)(2,1)} %bitcast.68) | data formatting | bytes 16777216 | tf_op jit(solution)/shard_map/all_to_all | solution.py:19
  1155.7 8.9 convert_bitcast_fusion
  1164.6 44.2 %copy.19 = bf16[32,32,128,32]{3,1,0,2:T(8,128)(2,1)} copy(bf16[32,32,128,32]{2,3,1,0:T(8,128)(2,1)} %convert_bitcast_fusion) | data formatting | bytes 16777216 | tf_op jit(solution)/shard_map/convert_element_type | solution.py:20
  1208.8 50.3 %reshape.10 = bf16[4,2,524288]{2,1,0:T(2,128)(2,1)} reshape(bf16[128,32,32,32]{3,2,1,0:T(8,128)(2,1)} %bitcast.62) | data formatting | bytes 16777216
  1259.1 100.5 %all_to_all.75 = bf16[4,2,524288]{2,1,0:T(2,128)(2,1)} all-to-all(bf16[4,2,524288]{2,1,0:T(2,128)(2,1)} %reshape.10), channel_id=1, replica_groups=mesh['fields'=2,'col'=4,'row'=4] {'row'}, dimensions={0} | all-to-all | bytes 16777216 | tf_op jit(solution)/shard_map/all_to_all | solution.py:21
  1359.6 36.9 %reshape.11 = bf16[128,32,32,32]{3,2,1,0:T(8,128)(2,1)} reshape(bf16[4,2,524288]{2,1,0:T(2,128)(2,1)} %all_to_all.75) | data formatting | bytes 16777216
  1396.5 51.1 %copy.20 = bf16[32,32,4,32,32]{1,2,4,3,0:T(4,128)(2,1)} copy(bf16[32,32,4,32,32]{4,1,0,3,2:T(8,128)(2,1)} %bitcast.69) | data formatting | bytes 16777216 | tf_op jit(solution)/shard_map/all_to_all | solution.py:21
  1447.5 0.0 copy-start.3
  1447.5 38.9 %all_to_all.67 = bf16[32,128,32,32]{1,3,2,0:T(8,128)(2,1)} reshape(bf16[32,4,32,32,32]{2,1,4,3,0:T(4,128)(2,1)} %bitcast.70) | data formatting | bytes 16777216 | tf_op jit(solution)/shard_map/all_to_all | solution.py:21
  1486.4 0.0 copy-done.3
  1486.4 11.9 convolution_bitcast_fusion
Async XLA Ops:
  0.0 331.3 %copy-start = (bf16[128,128]{1,0:T(8,128)(2,1)S(1)}, bf16[128,128]{1,0:T(8,128)(2,1)}, u32[]{:S(2)}) copy-start(bf16[128,128]{1,0:T(8,128)(2,1)} %param.7) | copy-start | bytes 98308
  704.9 38.9 %copy-start.1 = (f32[32,32,128]{2,1,0:T(8,128)S(1)}, f32[32,32,128]{2,1,0:T(8,128)}, u32[]{:S(2)}) copy-start(f32[32,32,128]{2,1,0:T(8,128)} %param.9) | copy-start | bytes 1572868
  704.9 38.9 %copy-start.2 = (bf16[128,128]{1,0:T(8,128)(2,1)S(1)}, bf16[128,128]{1,0:T(8,128)(2,1)}, u32[]{:S(2)}) copy-start(bf16[128,128]{1,0:T(8,128)(2,1)} %param.8) | copy-start | bytes 98308
  1447.5 38.9 %copy-start.3 = (bf16[128,128]{1,0:T(8,128)(2,1)S(1)}, bf16[128,128]{1,0:T(8,128)(2,1)}, u32[]{:S(2)}) copy-start(bf16[128,128]{1,0:T(8,128)(2,1)} %param.6) | copy-start | bytes 98308
where the time goes:
time: 1520 us; the launch traced here: 1500 us
  local copies, waits for them, and re-layouts  867 us (57%)
  blocking collectives  583 us (38%)
  matrix products  48 us (3%)
    unnamed x16, local copies, waits for them, and re-layouts  349 us
    all_to_all x1, blocking collectives, local_apply(): z_pencil = lax.all_to_all(stage_two, 'col', 2, 3, tiled=True)  191 us
    all_to_all x1, blocking collectives, local_apply(): back_y = lax.all_to_all(stage_four, 'col', 3, 2, tiled=True)  190 us
    all_to_all x1, blocking collectives, local_apply(): y_pencil = lax.all_to_all(stage_one, 'row', 1, 2, tiled=True)  101 us
    all_to_all x1, blocking collectives, local_apply(): back_x = lax.all_to_all(stage_five, 'row', 2, 1, tiled=True)  100 us
    all_to_all x2, local copies, waits for them, and re-layouts, local_apply(): back_x = lax.all_to_all(stage_five, 'row', 2, 1, tiled=True)  89.9 us
    all_to_all x2, local copies, waits for them, and re-layouts, local_apply(): y_pencil = lax.all_to_all(stage_one, 'row', 1, 2, tiled=True)  89.9 us
    all_to_all x2, local copies, waits for them, and re-layouts, local_apply(): z_pencil = lax.all_to_all(stage_two, 'col', 2, 3, tiled=True)  80.9 us

commit v1 on v0

v1 whole, which is shorter than its diff:
```python
import functools

import jax
import jax.numpy as jnp
from jax import lax
from jax.experimental import pallas as pl
from jax.experimental.pallas import tpu as pltpu
from jax.sharding import PartitionSpec as P

MESH = pl.DeviceIdType.MESH
N = 128
S = 32
PITCH = 136
GROUP = 4
F32, BF16 = jnp.float32, jnp.bfloat16

ORDER = [
    (0, 2), (2, 3), (1, 3), (3, 2), (0, 1), (2, 1), (2, 0),
    (1, 2), (3, 3), (0, 3), (2, 2), (1, 1), (3, 1), (3, 0), (1, 0),
]


def xor(value, bits):
    if bits == 0:
        return value
    if bits == 1:
        return value + 1 - 2 * lax.rem(value, 2)
    if bits == 2:
        return lax.rem(value + 2, 4)
    return 3 - value


def part(index):
    return pl.ds(pl.multiple_of(index * S, S), S)


def dot(lhs, rhs, lhs_dim, rhs_dim):
    return lax.dot_general(lhs, rhs, (((lhs_dim,), (rhs_dim,)), ((), ())), preferred_element_type=F32)


def exchange_kernel(
    u_ref, a_ref, b_ref, c_ref, d_ref, o_ref,
    tensors, scales, work, results, b_t,
    go_send, go_recv, d_send, d_recv, back_send, back_recv,
):
    row, col = lax.axis_index("row"), lax.axis_index("col")
    me = row * 4 + col

    def device(dr, dc):
        return {"row": xor(row, dr), "col": xor(col, dc)}

    def rank(dr, dc):
        return xor(row, dr) * 4 + xor(col, dc)

    barrier = pltpu.get_barrier_semaphore()
    for dr, dc in ORDER:
        pl.semaphore_signal(barrier, inc=1, device_id=device(dr, dc), device_id_type=MESH)
    pl.semaphore_wait(barrier, len(ORDER))

    def go(t, dr, dc):
        return pltpu.make_async_remote_copy(
            src_ref=u_ref.at[t * 16 + rank(dr, dc)],
            dst_ref=tensors.at[t, part(row), part(col), :],
            send_sem=go_send.at[t, dr * 4 + dc],
            recv_sem=go_recv.at[t, dr * 4 + dc],
            device_id=device(dr, dc),
            device_id_type=MESH,
        )

    def go_own(t):
        return pltpu.make_async_copy(
            u_ref.at[t * 16 + me], tensors.at[t, part(row), part(col), :], go_recv.at[t, 0]
        )

    def spread(slot, src, dst, dr, dc):
        return pltpu.make_async_remote_copy(
            src_ref=src, dst_ref=dst, send_sem=d_send.at[slot], recv_sem=d_recv.at[slot],
            device_id=device(dr, dc), device_id_type=MESH,
        )

    def back(t, dr, dc):
        return pltpu.make_async_remote_copy(
            src_ref=results.at[t, part(xor(row, dr)), part(xor(col, dc)), :],
            dst_ref=o_ref.at[t * 16 + me],
            send_sem=back_send.at[t, dr * 4 + dc],
            recv_sem=back_recv.at[t, dr * 4 + dc],
            device_id=device(dr, dc),
            device_id_type=MESH,
        )

    def back_own(t):
        return pltpu.make_async_copy(
            results.at[t, part(row), part(col), :], o_ref.at[t * 16 + me], back_recv.at[t, 0]
        )

    own_d = scales.at[part(row), part(col), :]
    far_d = scales.at[part(row), part(xor(col, 2)), :]
    row_d = scales.at[part(row)]
    far_row_d = scales.at[part(xor(row, 2))]
    keep_d = pltpu.make_async_copy(d_ref, own_d, d_recv.at[0])
    keep_d.start()
    steps = [
        [spread(1, d_ref, own_d, 0, 2)],
        [spread(2, d_ref, own_d, 0, 1), spread(3, far_d, far_d, 0, 1)],
        [spread(4, row_d, row_d, 2, 0)],
        [spread(5, row_d, row_d, 1, 0), spread(6, far_row_d, far_row_d, 1, 0)],
    ]
    cuts = [0, 4, 8, 15, 15]
    go_own(0).start()
    for n, step in enumerate(steps):
        for copy in step:
            copy.start()
        for dr, dc in ORDER[cuts[n]:cuts[n + 1]]:
            go(0, dr, dc).start()
        if n == 1:
            keep_d.wait()
        if n < 3:
            for copy in step:
                copy.wait_recv()
    go_own(1).start()
    for dr, dc in ORDER:
        go(1, dr, dc).start()

    b_t[...] = b_ref[...].T

    def first(step, t):
        pair = tensors[t, pl.ds(step * 2, 2)].reshape(2 * N, N)
        both = dot(a_ref[...], pair, 1, 1)
        for n in range(2):
            work[pl.ds(step * 2 + n, N, stride=PITCH), :] = both[:, n * N:(n + 1) * N]

    def chain(step, t):
        del t
        rows = [pl.ds(pl.multiple_of((step * GROUP + n) * PITCH, 8), N) for n in range(GROUP)]
        h1 = jnp.concatenate([work[r, :].astype(BF16) for r in rows], axis=1)
        h2 = dot(b_ref[...], h1, 1, 0).astype(BF16)
        h2 = jnp.concatenate([h2[:, n * N:(n + 1) * N] for n in range(GROUP)], axis=0)
        h3 = dot(h2, c_ref[...], 1, 1)
        h3 = (h3 * scales[pl.ds(step * GROUP, GROUP)].reshape(GROUP * N, N)).astype(BF16)
        h4 = dot(h3, c_ref[...], 1, 0).astype(BF16)
        h4 = jnp.concatenate([h4[n * N:(n + 1) * N] for n in range(GROUP)], axis=1)
        h5 = dot(b_t[...], h4, 1, 0)
        for n in range(GROUP):
            work[rows[n], :] = h5[:, n * N:(n + 1) * N]

    def turn(step, t, base):
        for n in range(2):
            y = base + step * 2 + n
            slab = work[pl.ds(y, N, stride=PITCH), :]
            results[t, y] = slab.T.astype(BF16)

    for t in range(2):
        go_own(t).wait()
        for dr, dc in ORDER:
            go(t, dr, dc).wait_recv()
        pl.loop(0, N // 2)(functools.partial(first, t=t))
        if t == 0:
            for copy in steps[3]:
                copy.wait_recv()
        pl.loop(0, N // GROUP)(functools.partial(chain, t=t))
        for dr in (2, 3, 1, 0):
            pl.loop(0, S // 2)(functools.partial(turn, t=t, base=xor(row, dr) * S))
            for dc in (2, 3, 1, 0):
                if (dr, dc) == (0, 0):
                    back_own(t).start()
                else:
                    back(t, dr, dc).start()

    for step in steps:
        for copy in step:
            copy.wait_send()
    for t in range(2):
        back_own(t).wait()
        for dr, dc in ORDER:
            go(t, dr, dc).wait_send()
            back(t, dr, dc).wait()


def last_kernel(h_ref, a_ref, w_ref):
    w_ref[...] = dot(h_ref[...], a_ref[...], 1, 0)


def solution(mesh):
    def local_apply(field_u, fac_a, fac_b, fac_c, diag_d):
        batch = field_u.shape[0]
        any_space = pl.BlockSpec(memory_space=pl.ANY)
        vmem = pl.BlockSpec(memory_space=pltpu.VMEM)
        h5 = pl.pallas_call(
            exchange_kernel,
            out_shape=jax.ShapeDtypeStruct((batch, S, S, N), BF16),
            in_specs=[any_space, vmem, vmem, vmem, any_space],
            out_specs=any_space,
            scratch_shapes=[
                pltpu.VMEM((2, N, N, N), BF16),
                pltpu.VMEM((N, N, N), F32),
                pltpu.VMEM((N * PITCH, N), F32),
                pltpu.VMEM((2, N, N, N), BF16),
                pltpu.VMEM((N, N), BF16),
                pltpu.SemaphoreType.DMA((2, 16)),
                pltpu.SemaphoreType.DMA((2, 16)),
                pltpu.SemaphoreType.DMA((7,)),
                pltpu.SemaphoreType.DMA((7,)),
                pltpu.SemaphoreType.DMA((2, 16)),
                pltpu.SemaphoreType.DMA((2, 16)),
            ],
            compiler_params=pltpu.CompilerParams(
                collective_id=0, has_side_effects=True, vmem_limit_bytes=60 * 2**20
            ),
            name="exchange",
        )(jnp.transpose(field_u, (0, 2, 3, 1)), fac_a, fac_b, fac_c, diag_d)
        rows = batch * S * S
        block = rows // 16
        w = pl.pallas_call(
            last_kernel,
            grid=(rows // block,),
            out_shape=jax.ShapeDtypeStruct((rows, N), F32),
            in_specs=[pl.BlockSpec((block, N), lambda n: (n, 0)), pl.BlockSpec((N, N), lambda n: (0, 0))],
            out_specs=pl.BlockSpec((block, N), lambda n: (n, 0)),
            name="last",
        )(h5.reshape(rows, N), fac_a)
        return jnp.transpose(w.reshape(batch, S, S, N), (0, 3, 1, 2))

    spec_field = P("fields", None, "row", "col")
    spec_factor = P("fields", None)
    return jax.shard_map(
        local_apply,
        mesh=mesh,
        in_specs=(spec_field, spec_factor, spec_factor, spec_factor, P(("fields", "row"), "col", None)),
        out_specs=spec_field,
        check_vma=False,
    )
```

time: 1520 us -> 424 us (0.28); the launches traced: 1500 us -> 422 us
  local copies, waits for them, and re-layouts: 867 us -> 0 us
  blocking collectives: 583 us -> 0 us
  Pallas kernels: 0 us -> 422 us
  matrix products: 48 us -> 0 us
    all_to_all x4 -> x0, blocking collectives: 583 us -> none  [the longest x1 191 us: local_apply(): z_pencil = lax.all_to_all(stage_two, 'col', 2, 3, tiled=True)]
    pallas_call x0 -> x2, Pallas kernels: none -> 422 us  [the longest x1 407 us: local_apply(): pl.pallas_call(exchange_kernel, out_shape=jax.ShapeDtypeStruct((batch, S,...]
    unnamed x16 -> x0, local copies, waits for them, and re-layouts: 349 us -> none
    all_to_all x8 -> x0, local copies, waits for them, and re-layouts: 342 us -> none  [the longest x2 89.9 us: local_apply(): back_x = lax.all_to_all(stage_five, 'row', 2, 1, tiled=True)]
    convert_element_type x4 -> x0, local copies, waits for them, and re-layouts: 177 us -> none  [the longest x1 44.2 us: local_apply(): jnp.einsum('ix,bxyz->biyz', fac_a, field_u, preferred_element_type=jnp.fl...]
    dot_general x5 -> x0, matrix products: 48 us -> none  [the longest x1 11.9 us: local_apply(): jnp.einsum('ix,biyz->bxyz', fac_a, back_x, preferred_element_type=jnp.flo...]
where the time goes in v1:
time: 424 us; the launch traced here: 422 us
  Pallas kernels  422 us (100%)
    pallas_call x1, Pallas kernels, local_apply(): pl.pallas_call(exchange_kernel, out_shape=jax.ShapeDtypeStruct((batch, S,...  407 us
    pallas_call x1, Pallas kernels, local_apply(): pl.pallas_call(last_kernel, grid=(rows // block,), out_shape=jax.ShapeDty...  15.1 us

profile of v1, /device:TPU:0, one launch (start us, length us, event | category | flops | bytes accessed | tf_op | source)
XLA Modules:
  0.0 422.5 jit_solution(2101316444307025466)
XLA Ops:
  0.0 407.4 %exchange.1 = bf16[32,32,32,128]{3,2,1,0:T(8,128)(2,1)} custom-call(bf16[32,32,32,128]{3,2,1,0:T(8,128)(2,1)} %bitcast.6, bf16[128,128]{1,0:T(8,128)(2,1)} %a_ref.3, bf16[128,128]{1,0:T(8,128)(2,1)} %b_ref.1, bf16[128,128]{1,0:T(8,128)(2,1)} %c_ref.1, f32[32,32,128]{2,1,0:T(8,128)} %d_ref.1), custom_call_target="tpu_custom_call" | custom-call | tf_op jit(solution)/shard_map/exchange/pallas_call | solution.py:188
  407.4 15.1 %last.1 = f32[32768,128]{1,0:T(8,128)} custom-call(bf16[32768,128]{1,0:T(8,128)(2,1)} %bitcast.5, bf16[128,128]{1,0:T(8,128)(2,1)} %a_ref.3), custom_call_target="tpu_custom_call" | custom-call | tf_op jit(solution)/shard_map/last/pallas_call | solution.py:213

commit v2 on v1

--- a/solution.py
+++ b/solution.py
@@ -92,6 +92,12 @@
         return pltpu.make_async_copy(
             results.at[t, part(row), part(col), :], o_ref.at[t * 16 + me], back_recv.at[t, 0]
         )
+
+    def send_back(t, dr, dc):
+        if (dr, dc) == (0, 0):
+            back_own(t).start()
+        else:
+            back(t, dr, dc).start()
 
     own_d = scales.at[part(row), part(col), :]
     far_d = scales.at[part(row), part(xor(col, 2)), :]
@@ -105,21 +111,20 @@
         [spread(4, row_d, row_d, 2, 0)],
         [spread(5, row_d, row_d, 1, 0), spread(6, far_row_d, far_row_d, 1, 0)],
     ]
-    cuts = [0, 4, 8, 15, 15]
+    sends = [(t, dr, dc) for t in range(2) for dr, dc in ORDER]
+    cuts = [0, 4, 8, 23, 30]
     go_own(0).start()
+    go_own(1).start()
     for n, step in enumerate(steps):
         for copy in step:
             copy.start()
-        for dr, dc in ORDER[cuts[n]:cuts[n + 1]]:
-            go(0, dr, dc).start()
+        for t, dr, dc in sends[cuts[n]:cuts[n + 1]]:
+            go(t, dr, dc).start()
         if n == 1:
             keep_d.wait()
         if n < 3:
             for copy in step:
                 copy.wait_recv()
-    go_own(1).start()
-    for dr, dc in ORDER:
-        go(1, dr, dc).start()
 
     b_t[...] = b_ref[...].T
 
@@ -160,11 +165,12 @@
         pl.loop(0, N // GROUP)(functools.partial(chain, t=t))
         for dr in (2, 3, 1, 0):
             pl.loop(0, S // 2)(functools.partial(turn, t=t, base=xor(row, dr) * S))
-            for dc in (2, 3, 1, 0):
-                if (dr, dc) == (0, 0):
-                    back_own(t).start()
-                else:
-                    back(t, dr, dc).start()
+            if t == 0:
+                for dc in (2, 3, 1, 0):
+                    send_back(t, dr, dc)
+    for dc in (1, 0, 2, 3):
+        for dr in (2, 3, 1, 0):
+            send_back(1, dr, dc)
 
     for step in steps:
         for copy in step:
@@ -177,7 +183,9 @@
 
 
 def last_kernel(h_ref, a_ref, w_ref):
-    w_ref[...] = dot(h_ref[...], a_ref[...], 1, 0)
+    rows = w_ref.shape[0]
+    start = pl.multiple_of(pl.program_id(0) * rows, rows)
+    w_ref[...] = dot(h_ref[pl.ds(start, rows), :], a_ref[...], 1, 0)
 
 
 def solution(mesh):
@@ -204,7 +212,7 @@
                 pltpu.SemaphoreType.DMA((2, 16)),
             ],
             compiler_params=pltpu.CompilerParams(
-                collective_id=0, has_side_effects=True, vmem_limit_bytes=60 * 2**20
+                collective_id=0, has_side_effects=True, vmem_limit_bytes=44 * 2**20
             ),
             name="exchange",
         )(jnp.transpose(field_u, (0, 2, 3, 1)), fac_a, fac_b, fac_c, diag_d)
@@ -214,8 +222,9 @@
             last_kernel,
             grid=(rows // block,),
             out_shape=jax.ShapeDtypeStruct((rows, N), F32),
-            in_specs=[pl.BlockSpec((block, N), lambda n: (n, 0)), pl.BlockSpec((N, N), lambda n: (0, 0))],
+            in_specs=[vmem, vmem],
             out_specs=pl.BlockSpec((block, N), lambda n: (n, 0)),
+            compiler_params=pltpu.CompilerParams(vmem_limit_bytes=24 * 2**20),
             name="last",
         )(h5.reshape(rows, N), fac_a)
         return jnp.transpose(w.reshape(batch, S, S, N), (0, 3, 1, 2))

time: 424 us -> 408 us (0.962)
  the two profiles are of different devices: /device:TPU:0 before, /device:TPU:18 now
where the time goes in v2:
time: 408 us
  Pallas kernels  404 us (99%)
    pallas_call x1, Pallas kernels, local_apply(): pl.pallas_call(exchange_kernel, out_shape=jax.ShapeDtypeStruct((batch, S,...  394 us
    pallas_call x1, Pallas kernels, local_apply(): pl.pallas_call(last_kernel, grid=(rows // block,), out_shape=jax.ShapeDty...  10.3 us

profile of v2, /device:TPU:18, one launch (start us, length us, event | category | flops | bytes accessed | tf_op | source)
XLA Modules:
  0.0 407.6 jit_solution(10911282234385640657)
XLA Ops:
  0.0 0.0 copy-start
  0.0 1.0 copy-done
  1.0 0.0 copy-start.1
  1.0 0.8 copy-done.1
  1.8 0.0 copy-start.2
  1.8 0.8 copy-done.2
  2.6 0.0 copy-start.3
  2.6 0.8 copy-done.3
  3.3 393.9 %exchange.1 = bf16[32,32,32,128]{3,2,1,0:T(8,128)(2,1)S(1)} custom-call(bf16[32,32,32,128]{3,2,1,0:T(8,128)(2,1)} %bitcast.6, bf16[128,128]{1,0:T(8,128)(2,1)S(1)} %copy-done.1, bf16[128,128]{1,0:T(8,128)(2,1)S(1)} %copy-done.2, bf16[128,128]{1,0:T(8,128)(2,1)S(1)} %copy-done.3, f32[32,32,128]{2,1,0:T(8,128)S(1)} %copy-done), custom_call_target="tpu_custom_call" | custom-call | tf_op jit(solution)/shard_map/exchange/pallas_call | solution.py:196
  397.3 10.3 %last.1 = f32[32768,128]{1,0:T(8,128)} custom-call(bf16[32768,128]{1,0:T(8,128)(2,1)S(1)} %bitcast.5, bf16[128,128]{1,0:T(8,128)(2,1)S(1)} %copy-done.1), custom_call_target="tpu_custom_call" | custom-call | tf_op jit(solution)/shard_map/last/pallas_call | solution.py:221
Async XLA Ops:
  0.0 1.0 copy-start
  1.0 0.8 copy-start.1
  1.8 0.8 copy-start.2
  2.6 0.8 copy-start.3

commit v3 on v2

--- a/solution.py
+++ b/solution.py
@@ -12,6 +12,7 @@
 S = 32
 PITCH = 136
 GROUP = 4
+BLOCKS, BLOCK = 32, 1024
 F32, BF16 = jnp.float32, jnp.bfloat16
 
 ORDER = [
@@ -39,8 +40,8 @@
 
 
 def exchange_kernel(
-    u_ref, a_ref, b_ref, c_ref, d_ref, o_ref,
-    tensors, scales, work, results, b_t,
+    u_ref, a_hbm, b_hbm, c_hbm, d_ref, o_ref, a_out,
+    tensors, scales, work, results, a_ref, b_ref, c_ref, b_t, factor_sem,
     go_send, go_recv, d_send, d_recv, back_send, back_recv,
 ):
     row, col = lax.axis_index("row"), lax.axis_index("col")
@@ -52,6 +53,12 @@
     def rank(dr, dc):
         return xor(row, dr) * 4 + xor(col, dc)
 
+    factors = [
+        pltpu.make_async_copy(a_hbm, a_ref, factor_sem.at[0]),
+        pltpu.make_async_copy(b_hbm, b_ref, factor_sem.at[1]),
+        pltpu.make_async_copy(c_hbm, c_ref, factor_sem.at[2]),
+        pltpu.make_async_copy(a_hbm, a_out, factor_sem.at[3]),
+    ]
     barrier = pltpu.get_barrier_semaphore()
     for dr, dc in ORDER:
         pl.semaphore_signal(barrier, inc=1, device_id=device(dr, dc), device_id_type=MESH)
@@ -126,6 +133,10 @@
             for copy in step:
                 copy.wait_recv()
 
+    for copy in factors:
+        copy.start()
+    for copy in factors:
+        copy.wait()
     b_t[...] = b_ref[...].T
 
     def first(step, t):
@@ -182,10 +193,20 @@
             back(t, dr, dc).wait()
 
 
-def last_kernel(h_ref, a_ref, w_ref):
-    rows = w_ref.shape[0]
-    start = pl.multiple_of(pl.program_id(0) * rows, rows)
-    w_ref[...] = dot(h_ref[pl.ds(start, rows), :], a_ref[...], 1, 0)
+def last_kernel(h_ref, a_ref, w_ref, out, sem):
+    def store(n):
+        rows = pl.ds(pl.multiple_of(n * BLOCK, BLOCK), BLOCK)
+        return pltpu.make_async_copy(out.at[rows], w_ref.at[rows], sem.at[n])
+
+    @pl.loop(0, BLOCKS)
+    def _(n):
+        rows = pl.ds(pl.multiple_of(n * BLOCK, BLOCK), BLOCK)
+        out[rows, :] = dot(h_ref[rows, :], a_ref[...], 1, 0)
+        store(n).start()
+
+    @pl.loop(0, BLOCKS)
+    def _(n):
+        store(n).wait()
 
 
 def solution(mesh):
@@ -193,17 +214,26 @@
         batch = field_u.shape[0]
         any_space = pl.BlockSpec(memory_space=pl.ANY)
         vmem = pl.BlockSpec(memory_space=pltpu.VMEM)
-        h5 = pl.pallas_call(
+
+        def in_hbm(array):
+            return pltpu.with_memory_space_constraint(array, pltpu.HBM)
+
+        operands = (jnp.transpose(field_u, (0, 2, 3, 1)), fac_a, fac_b, fac_c, diag_d)
+        h5, last_a = pl.pallas_call(
             exchange_kernel,
-            out_shape=jax.ShapeDtypeStruct((batch, S, S, N), BF16),
-            in_specs=[any_space, vmem, vmem, vmem, any_space],
-            out_specs=any_space,
+            out_shape=(pltpu.VMEM((batch, S, S, N), BF16), pltpu.VMEM((N, N), BF16)),
+            in_specs=[any_space] * 5,
+            out_specs=(any_space, any_space),
             scratch_shapes=[
                 pltpu.VMEM((2, N, N, N), BF16),
                 pltpu.VMEM((N, N, N), F32),
                 pltpu.VMEM((N * PITCH, N), F32),
                 pltpu.VMEM((2, N, N, N), BF16),
                 pltpu.VMEM((N, N), BF16),
+                pltpu.VMEM((N, N), BF16),
+                pltpu.VMEM((N, N), BF16),
+                pltpu.VMEM((N, N), BF16),
+                pltpu.SemaphoreType.DMA((4,)),
                 pltpu.SemaphoreType.DMA((2, 16)),
                 pltpu.SemaphoreType.DMA((2, 16)),
                 pltpu.SemaphoreType.DMA((7,)),
@@ -215,18 +245,16 @@
                 collective_id=0, has_side_effects=True, vmem_limit_bytes=44 * 2**20
             ),
             name="exchange",
-        )(jnp.transpose(field_u, (0, 2, 3, 1)), fac_a, fac_b, fac_c, diag_d)
-        rows = batch * S * S
-        block = rows // 16
+        )(*(in_hbm(operand) for operand in operands))
         w = pl.pallas_call(
             last_kernel,
-            grid=(rows // block,),
-            out_shape=jax.ShapeDtypeStruct((rows, N), F32),
+            out_shape=jax.ShapeDtypeStruct((BLOCKS * BLOCK, N), F32),
             in_specs=[vmem, vmem],
-            out_specs=pl.BlockSpec((block, N), lambda n: (n, 0)),
+            out_specs=any_space,
+            scratch_shapes=[pltpu.VMEM((BLOCKS * BLOCK, N), F32), pltpu.SemaphoreType.DMA((BLOCKS,))],
             compiler_params=pltpu.CompilerParams(vmem_limit_bytes=24 * 2**20),
             name="last",
-        )(h5.reshape(rows, N), fac_a)
+        )(h5.reshape(BLOCKS * BLOCK, N), last_a)
         return jnp.transpose(w.reshape(batch, S, S, N), (0, 3, 1, 2))
 
     spec_field = P("fields", None, "row", "col")

time: 408 us -> 402 us (0.985)
  the two profiles are of different devices: /device:TPU:18 before, /device:TPU:22 now
where the time goes in v3:
time: 402 us
  Pallas kernels  402 us (100%)
    pallas_call x1, Pallas kernels, local_apply(): pl.pallas_call(exchange_kernel, out_shape=(pltpu.VMEM((batch, S, S, N), B...  394 us

profile of v3, /device:TPU:22, one launch (start us, length us, event | category | flops | bytes accessed | tf_op | source)
XLA Modules:
  0.0 401.9 jit_solution(6645790056868913033)
XLA Ops:
  0.0 394.0 %exchange.1 = (bf16[32,32,32,128]{3,2,1,0:T(8,128)(2,1)S(1)}, bf16[128,128]{1,0:T(8,128)(2,1)S(1)}) custom-call(bf16[32,32,32,128]{3,2,1,0:T(8,128)(2,1)} %bitcast.6, bf16[128,128]{1,0:T(8,128)(2,1)} %a_hbm.1, bf16[128,128]{1,0:T(8,128)(2,1)} %b_hbm.1, bf16[128,128]{1,0:T(8,128)(2,1)} %c_hbm.1, f32[32,32,128]{2,1,0:T(8,128)} %d_ref.1), custom_call_target="tpu_custom_call" | custom-call | tf_op jit(solution)/shard_map/exchange/pallas_call | solution.py:222
  394.1 7.8 %last.1 = f32[32768,128]{1,0:T(8,128)} custom-call(bf16[32768,128]{1,0:T(8,128)(2,1)S(1)} %bitcast.5, bf16[128,128]{1,0:T(8,128)(2,1)S(1)} %get-tuple-element.8.a_ref), custom_call_target="tpu_custom_call" | custom-call | tf_op jit(solution)/shard_map/last/pallas_call | solution.py:249

commit v4 on v0

v4 whole, which is shorter than its diff:
```python
import functools

import jax
import jax.numpy as jnp
from jax import lax
from jax.experimental import pallas as pl
from jax.experimental.pallas import tpu as pltpu
from jax.sharding import PartitionSpec as P

MESH = pl.DeviceIdType.MESH
N = 128
S = 32
H = 16
ROUNDS = 8
UNITS = 2 * ROUNDS
GROUP = 4
BLOCKS, BLOCK = 32, 1024
F32, BF16 = jnp.float32, jnp.bfloat16
PEERS = (1, 2, 3)


def xor(value, bits):
    if bits == 0:
        return value
    if bits == 1:
        return value + 1 - 2 * lax.rem(value, 2)
    if bits == 2:
        return lax.rem(value + 2, 4)
    return 3 - value


def chunk(index, size=S):
    return pl.ds(pl.multiple_of(index * size, size), size)


def dot(lhs, rhs, lhs_dim, rhs_dim):
    return lax.dot_general(lhs, rhs, (((lhs_dim,), (rhs_dim,)), ((), ())), preferred_element_type=F32)


def exchange_kernel(
    u_ref, a_hbm, b_hbm, c_hbm, d_ref, o_ref, a_out,
    tens, cols, rets, front, rear, diag, diag_t, a_ref, b_ref, c_ref, b_t, c_t, factor_sem,
    d_send, d_recv, row_send, row_recv, go_send, go_recv, back_send, back_recv, home_send, home_recv,
):
    row, col = lax.axis_index("row"), lax.axis_index("col")

    def copy(src, dst, send, recv, peer):
        if not peer:
            return pltpu.make_async_copy(src, dst, recv)
        return pltpu.make_async_remote_copy(
            src_ref=src, dst_ref=dst, send_sem=send, recv_sem=recv, device_id=peer, device_id_type=MESH
        )

    def row_peer(dr):
        return {"row": xor(row, dr), "col": col} if dr else None

    def col_peer(dc):
        return {"row": row, "col": xor(col, dc)} if dc else None

    def halves(unit):
        return lax.div(unit, 2), lax.rem(unit, 2)

    def row_copy(unit, dr):
        t, z = halves(unit)
        return copy(
            u_ref.at[t * 4 + xor(row, dr), :, chunk(z, H), :], tens.at[unit, chunk(row)],
            row_send.at[unit, dr], row_recv.at[unit, dr], row_peer(dr),
        )

    def go_copy(unit, dc):
        t, z = halves(unit)
        return copy(
            tens.at[unit, chunk(xor(col, dc))], cols.at[t, :, chunk(col * 2 + z, H), :],
            go_send.at[unit, dc], go_recv.at[unit, dc], col_peer(dc),
        )

    def back_copy(unit, dc):
        t, z = halves(unit)
        return copy(
            cols.at[t, :, chunk(xor(col, dc) * 2 + z, H), :], rets.at[unit, chunk(col)],
            back_send.at[unit, dc], back_recv.at[unit, dc], col_peer(dc),
        )

    def home_copy(unit, dr):
        t, z = halves(unit)
        return copy(
            rets.at[unit, chunk(xor(row, dr))], o_ref.at[t * 4 + row, :, chunk(z, H), :],
            home_send.at[unit, dr], home_recv.at[unit, dr], row_peer(dr),
        )

    def start(kind, unit):
        for peer in (*PEERS, 0):
            kind(unit, peer).start()

    def arrive(kind, unit):
        kind(unit, 0).wait()
        for peer in PEERS:
            kind(unit, peer).wait_recv()

    barrier = pltpu.get_barrier_semaphore()
    for peer in PEERS:
        pl.semaphore_signal(barrier, inc=1, device_id=row_peer(peer), device_id_type=MESH)
        pl.semaphore_signal(barrier, inc=1, device_id=col_peer(peer), device_id_type=MESH)
    pl.semaphore_wait(barrier, 2 * len(PEERS))

    @pl.loop(0, 4)
    def _(unit):
        start(row_copy, unit)

    own_d, far_d = diag.at[chunk(row, S * S)], diag.at[chunk(xor(row, 2), S * S)]
    keep_d = copy(d_ref, own_d, None, d_recv.at[0], None)
    cross_d = copy(d_ref, own_d, d_send.at[1], d_recv.at[1], row_peer(2))
    near_d = copy(d_ref, own_d, d_send.at[2], d_recv.at[2], row_peer(1))
    pass_d = copy(far_d, far_d, d_send.at[3], d_recv.at[3], row_peer(1))
    for start_d in (cross_d, near_d, keep_d):
        start_d.start()

    @pl.loop(4, 8)
    def _(unit):
        start(row_copy, unit)

    factors = [
        pltpu.make_async_copy(a_hbm, a_ref, factor_sem.at[0]),
        pltpu.make_async_copy(b_hbm, b_ref, factor_sem.at[1]),
        pltpu.make_async_copy(c_hbm, c_ref, factor_sem.at[2]),
        pltpu.make_async_copy(a_hbm, a_out, factor_sem.at[3]),
    ]
    for factor in factors:
        factor.start()
    for factor in factors:
        factor.wait()
    b_t[...] = b_ref[...].T
    c_t[...] = c_ref[...].T

    def swapped(matrix):
        @pl.loop(0, H // GROUP)
        def _(step):
            lines = [pl.ds(step * GROUP + n, N, stride=H) for n in range(GROUP)]
            side = jnp.concatenate([front[line, :].astype(BF16) for line in lines], axis=1)
            both = dot(matrix[...], side, 1, 0)
            for n, line in enumerate(lines):
                rear[line, :] = both[:, n * N:(n + 1) * N]

    def rounded(buffer, unit):
        @pl.loop(0, 4)
        def _(q):
            buffer[unit, chunk(q)] = rear[chunk(q, S * H), :].reshape(S, H, N).astype(BF16)

    def first_two(unit):
        arrive(row_copy, unit)

        @pl.loop(0, 4)
        def _(q):
            front[chunk(q, S * H), :] = dot(tens[unit, chunk(q)].reshape(S * H, N), a_ref[...], 1, 1)

        swapped(b_ref)
        rounded(tens, unit)
        start(go_copy, unit)

    def middle(t):
        arrive(go_copy, 2 * t)
        arrive(go_copy, 2 * t + 1)

        @pl.loop(0, S // GROUP)
        def _(step):
            def side(buffer):
                return jnp.concatenate([buffer[step * GROUP + n] for n in range(GROUP)], axis=1)

            h3 = (dot(c_ref[...], side(cols.at[t]), 1, 0) * side(diag_t)).astype(BF16)
            h4 = dot(c_t[...], h3, 1, 0).astype(BF16)
            for n in range(GROUP):
                cols[t, step * GROUP + n] = h4[:, n * N:(n + 1) * N]

        start(back_copy, 2 * t)
        start(back_copy, 2 * t + 1)

    def fifth(unit):
        arrive(back_copy, unit)

        @pl.loop(0, 4)
        def _(q):
            front[chunk(q, S * H), :] = rets[unit, chunk(q)].reshape(S * H, N).astype(F32)

        swapped(b_t)
        rounded(rets, unit)
        start(home_copy, unit)

    pl.loop(0, 4)(first_two)
    cross_d.wait_recv()
    pass_d.start()
    keep_d.wait()
    near_d.wait_recv()
    pass_d.wait_recv()

    @pl.loop(0, S)
    def _(j):
        diag_t[j] = diag[pl.ds(j, N, stride=S), :].T

    def body(t, rows, firsts, fifths):
        middle(t)
        if rows:
            start(row_copy, 2 * t + 8)
            start(row_copy, 2 * t + 9)
        if firsts:
            pl.loop(2 * t + 4, 2 * t + 6)(first_two)
        if fifths:
            pl.loop(2 * t - 2, 2 * t)(fifth)

    pl.loop(0, 1)(functools.partial(body, rows=True, firsts=True, fifths=False))
    pl.loop(1, 4)(functools.partial(body, rows=True, firsts=True, fifths=True))
    pl.loop(4, 6)(functools.partial(body, rows=False, firsts=True, fifths=True))
    pl.loop(6, 8)(functools.partial(body, rows=False, firsts=False, fifths=True))
    pl.loop(14, 16)(fifth)

    for sent in (cross_d, near_d, pass_d):
        sent.wait_send()

    @pl.loop(0, UNITS)
    def _(unit):
        arrive(home_copy, unit)
        for kind in (row_copy, go_copy, back_copy, home_copy):
            for peer in PEERS:
                kind(unit, peer).wait_send()


def last_kernel(h_ref, a_ref, w_ref, out, sem):
    def store(n):
        rows = chunk(n, BLOCK)
        return pltpu.make_async_copy(out.at[rows], w_ref.at[rows], sem.at[n])

    @pl.loop(0, BLOCKS)
    def _(n):
        rows = chunk(n, BLOCK)
        out[rows, :] = dot(h_ref[rows, :], a_ref[...], 1, 0)
        store(n).start()

    @pl.loop(0, BLOCKS)
    def _(n):
        store(n).wait()


def solution(mesh):
    def local_apply(field_u, fac_a, fac_b, fac_c, diag_d):
        batch = field_u.shape[0]
        any_space = pl.BlockSpec(memory_space=pl.ANY)
        vmem = pl.BlockSpec(memory_space=pltpu.VMEM)

        def in_hbm(array):
            return pltpu.with_memory_space_constraint(array, pltpu.HBM)

        operands = (jnp.transpose(field_u, (0, 2, 3, 1)), fac_a, fac_b, fac_c, diag_d.reshape(S * S, N))
        pairs = pltpu.SemaphoreType.DMA((UNITS, 4))
        h5, last_a = pl.pallas_call(
            exchange_kernel,
            out_shape=(pltpu.VMEM((batch, S, S, N), BF16), pltpu.VMEM((N, N), BF16)),
            in_specs=[any_space] * 5,
            out_specs=(any_space, any_space),
            scratch_shapes=[
                pltpu.VMEM((UNITS, N, H, N), BF16),
                pltpu.VMEM((ROUNDS, S, N, N), BF16),
                pltpu.VMEM((UNITS, N, H, N), BF16),
                pltpu.VMEM((N * H, N), F32),
                pltpu.VMEM((N * H, N), F32),
                pltpu.VMEM((N * S, N), F32),
                pltpu.VMEM((S, N, N), F32),
                pltpu.VMEM((N, N), BF16),
                pltpu.VMEM((N, N), BF16),
                pltpu.VMEM((N, N), BF16),
                pltpu.VMEM((N, N), BF16),
                pltpu.VMEM((N, N), BF16),
                pltpu.SemaphoreType.DMA((4,)),
                pltpu.SemaphoreType.DMA((4,)),
                pltpu.SemaphoreType.DMA((4,)),
                pairs, pairs, pairs, pairs, pairs, pairs, pairs, pairs,
            ],
            compiler_params=pltpu.CompilerParams(
                collective_id=0, has_side_effects=True, vmem_limit_bytes=44 * 2**20
            ),
            name="exchange",
        )(*(in_hbm(operand) for operand in operands))
        w = pl.pallas_call(
            last_kernel,
            out_shape=jax.ShapeDtypeStruct((BLOCKS * BLOCK, N), F32),
            in_specs=[vmem, vmem],
            out_specs=any_space,
            scratch_shapes=[pltpu.VMEM((BLOCKS * BLOCK, N), F32), pltpu.SemaphoreType.DMA((BLOCKS,))],
            compiler_params=pltpu.CompilerParams(vmem_limit_bytes=24 * 2**20),
            name="last",
        )(h5.reshape(BLOCKS * BLOCK, N), last_a)
        return jnp.transpose(w.reshape(batch, S, S, N), (0, 3, 1, 2))

    spec_field = P("fields", None, "row", "col")
    spec_factor = P("fields", None)
    return jax.shard_map(
        local_apply,
        mesh=mesh,
        in_specs=(spec_field, spec_factor, spec_factor, spec_factor, P(("fields", "row"), "col", None)),
        out_specs=spec_field,
        check_vma=False,
    )
```

time: 1520 us -> 397 us (0.26); the launches traced: 1500 us -> 396 us
  local copies, waits for them, and re-layouts: 867 us -> 0 us
  blocking collectives: 583 us -> 0 us
  Pallas kernels: 0 us -> 396 us
  matrix products: 48 us -> 0 us
    all_to_all x4 -> x0, blocking collectives: 583 us -> none  [the longest x1 191 us: local_apply(): z_pencil = lax.all_to_all(stage_two, 'col', 2, 3, tiled=True)]
    pallas_call x0 -> x2, Pallas kernels: none -> 396 us  [the longest x1 388 us: local_apply(): pl.pallas_call(exchange_kernel, out_shape=(pltpu.VMEM((batch, S, S, N), B...]
    unnamed x16 -> x0, local copies, waits for them, and re-layouts: 349 us -> none
    all_to_all x8 -> x0, local copies, waits for them, and re-layouts: 342 us -> none  [the longest x2 89.9 us: local_apply(): back_x = lax.all_to_all(stage_five, 'row', 2, 1, tiled=True)]
    convert_element_type x4 -> x0, local copies, waits for them, and re-layouts: 177 us -> none  [the longest x1 44.2 us: local_apply(): jnp.einsum('ix,bxyz->biyz', fac_a, field_u, preferred_element_type=jnp.fl...]
    dot_general x5 -> x0, matrix products: 48 us -> none  [the longest x1 11.9 us: local_apply(): jnp.einsum('ix,biyz->bxyz', fac_a, back_x, preferred_element_type=jnp.flo...]
where the time goes in v4:
time: 397 us; the launch traced here: 396 us
  Pallas kernels  396 us (100%)
    pallas_call x1, Pallas kernels, local_apply(): pl.pallas_call(exchange_kernel, out_shape=(pltpu.VMEM((batch, S, S, N), B...  388 us

profile of v4, /device:TPU:0, one launch (start us, length us, event | category | flops | bytes accessed | tf_op | source)
XLA Modules:
  0.0 395.7 jit_solution(2175764814483847340)
XLA Ops:
  0.0 387.9 %exchange.1 = (bf16[32,32,32,128]{3,2,1,0:T(8,128)(2,1)S(1)}, bf16[128,128]{1,0:T(8,128)(2,1)S(1)}) custom-call(bf16[32,32,32,128]{3,2,1,0:T(8,128)(2,1)} %bitcast.7, bf16[128,128]{1,0:T(8,128)(2,1)} %a_hbm.1, bf16[128,128]{1,0:T(8,128)(2,1)} %b_hbm.1, bf16[128,128]{1,0:T(8,128)(2,1)} %c_hbm.1, f32[1024,128]{1,0:T(8,128)} %bitcast.8), custom_call_target="tpu_custom_call" | custom-call | tf_op jit(solution)/shard_map/exchange/pallas_call | solution.py:253
  387.9 7.8 %last.1 = f32[32768,128]{1,0:T(8,128)} custom-call(bf16[32768,128]{1,0:T(8,128)(2,1)S(1)} %bitcast.6, bf16[128,128]{1,0:T(8,128)(2,1)S(1)} %get-tuple-element.8.a_ref), custom_call_target="tpu_custom_call" | custom-call | tf_op jit(solution)/shard_map/last/pallas_call | solution.py:281

commit v5 on v4

--- a/solution.py
+++ b/solution.py
@@ -10,11 +10,12 @@
 MESH = pl.DeviceIdType.MESH
 N = 128
 S = 32
-H = 16
+H = 8
+PER = S // H
 ROUNDS = 8
-UNITS = 2 * ROUNDS
+UNITS = PER * ROUNDS
 GROUP = 4
-BLOCKS, BLOCK = 32, 1024
+BLOCKS, BLOCK = 16, 2048
 F32, BF16 = jnp.float32, jnp.bfloat16
 PEERS = (1, 2, 3)
 
@@ -58,7 +59,7 @@
         return {"row": row, "col": xor(col, dc)} if dc else None
 
     def halves(unit):
-        return lax.div(unit, 2), lax.rem(unit, 2)
+        return lax.div(unit, PER), lax.rem(unit, PER)
 
     def row_copy(unit, dr):
         t, z = halves(unit)
@@ -70,14 +71,14 @@
     def go_copy(unit, dc):
         t, z = halves(unit)
         return copy(
-            tens.at[unit, chunk(xor(col, dc))], cols.at[t, :, chunk(col * 2 + z, H), :],
+            tens.at[unit, chunk(xor(col, dc))], cols.at[t, :, chunk(col * PER + z, H), :],
             go_send.at[unit, dc], go_recv.at[unit, dc], col_peer(dc),
         )
 
     def back_copy(unit, dc):
         t, z = halves(unit)
         return copy(
-            cols.at[t, :, chunk(xor(col, dc) * 2 + z, H), :], rets.at[unit, chunk(col)],
+            cols.at[t, :, chunk(xor(col, dc) * PER + z, H), :], rets.at[unit, chunk(col)],
             back_send.at[unit, dc], back_recv.at[unit, dc], col_peer(dc),
         )
 
@@ -89,7 +90,7 @@
         )
 
     def start(kind, unit):
-        for peer in (*PEERS, 0):
+        for peer in (0, 3, 2, 1) if kind in (row_copy, home_copy) else (1, 2, 3, 0):
             kind(unit, peer).start()
 
     def arrive(kind, unit):
@@ -103,7 +104,7 @@
         pl.semaphore_signal(barrier, inc=1, device_id=col_peer(peer), device_id_type=MESH)
     pl.semaphore_wait(barrier, 2 * len(PEERS))
 
-    @pl.loop(0, 4)
+    @pl.loop(0, 2 * PER)
     def _(unit):
         start(row_copy, unit)
 
@@ -115,7 +116,7 @@
     for start_d in (cross_d, near_d, keep_d):
         start_d.start()
 
-    @pl.loop(4, 8)
+    @pl.loop(2 * PER, 4 * PER)
     def _(unit):
         start(row_copy, unit)
 
@@ -158,8 +159,8 @@
         start(go_copy, unit)
 
     def middle(t):
-        arrive(go_copy, 2 * t)
-        arrive(go_copy, 2 * t + 1)
+        for n in range(PER):
+            arrive(go_copy, PER * t + n)
 
         @pl.loop(0, S // GROUP)
         def _(step):
@@ -171,8 +172,8 @@
             for n in range(GROUP):
                 cols[t, step * GROUP + n] = h4[:, n * N:(n + 1) * N]
 
-        start(back_copy, 2 * t)
-        start(back_copy, 2 * t + 1)
+        for n in range(PER):
+            start(back_copy, PER * t + n)
 
     def fifth(unit):
         arrive(back_copy, unit)
@@ -185,7 +186,7 @@
         rounded(rets, unit)
         start(home_copy, unit)
 
-    pl.loop(0, 4)(first_two)
+    pl.loop(0, 2 * PER)(first_two)
     cross_d.wait_recv()
     pass_d.start()
     keep_d.wait()
@@ -199,18 +200,18 @@
     def body(t, rows, firsts, fifths):
         middle(t)
         if rows:
-            start(row_copy, 2 * t + 8)
-            start(row_copy, 2 * t + 9)
+            for n in range(PER):
+                start(row_copy, PER * (t + 4) + n)
         if firsts:
-            pl.loop(2 * t + 4, 2 * t + 6)(first_two)
+            pl.loop(PER * (t + 2), PER * (t + 3))(first_two)
         if fifths:
-            pl.loop(2 * t - 2, 2 * t)(fifth)
+            pl.loop(PER * (t - 1), PER * t)(fifth)
 
     pl.loop(0, 1)(functools.partial(body, rows=True, firsts=True, fifths=False))
     pl.loop(1, 4)(functools.partial(body, rows=True, firsts=True, fifths=True))
     pl.loop(4, 6)(functools.partial(body, rows=False, firsts=True, fifths=True))
     pl.loop(6, 8)(functools.partial(body, rows=False, firsts=False, fifths=True))
-    pl.loop(14, 16)(fifth)
+    pl.loop(PER * 7, PER * 8)(fifth)
 
     for sent in (cross_d, near_d, pass_d):
         sent.wait_send()

time: 397 us -> 397 us (level)
  no operation moved by 1% of the time
where the time goes in v5:
time: 397 us; the launch traced here: 395 us
  Pallas kernels  395 us (99%)
    pallas_call x1, Pallas kernels, local_apply(): pl.pallas_call(exchange_kernel, out_shape=(pltpu.VMEM((batch, S, S, N), B...  389 us

profile of v5, /device:TPU:0, one launch (start us, length us, event | category | flops | bytes accessed | tf_op | source)
XLA Modules:
  0.0 395.1 jit_solution(5387115211094621204)
XLA Ops:
  0.0 388.9 %exchange.1 = (bf16[32,32,32,128]{3,2,1,0:T(8,128)(2,1)S(1)}, bf16[128,128]{1,0:T(8,128)(2,1)S(1)}) custom-call(bf16[32,32,32,128]{3,2,1,0:T(8,128)(2,1)} %bitcast.7, bf16[128,128]{1,0:T(8,128)(2,1)} %a_hbm.1, bf16[128,128]{1,0:T(8,128)(2,1)} %b_hbm.1, bf16[128,128]{1,0:T(8,128)(2,1)} %c_hbm.1, f32[1024,128]{1,0:T(8,128)} %bitcast.8), custom_call_target="tpu_custom_call" | custom-call | tf_op jit(solution)/shard_map/exchange/pallas_call | solution.py:254
  388.9 6.2 %last.1 = f32[32768,128]{1,0:T(8,128)} custom-call(bf16[32768,128]{1,0:T(8,128)(2,1)S(1)} %bitcast.6, bf16[128,128]{1,0:T(8,128)(2,1)S(1)} %get-tuple-element.8.a_ref), custom_call_target="tpu_custom_call" | custom-call | tf_op jit(solution)/shard_map/last/pallas_call | solution.py:282

commit v6 on v4

v6 whole, which is shorter than its diff:
```python
import functools

import jax
import jax.numpy as jnp
from jax import lax
from jax.experimental import pallas as pl
from jax.experimental.pallas import tpu as pltpu
from jax.sharding import PartitionSpec as P

MESH = pl.DeviceIdType.MESH
N = 128
S = 32
H = 16
FINE = 8
PER = S // FINE
ROUNDS = 8
EARLY = 2
LATE = 1
GROUP = 4
BLOCKS, BLOCK = 8, 4096
F32, BF16 = jnp.float32, jnp.bfloat16
PEERS = (1, 2, 3)


def xor(value, bits):
    if bits == 0:
        return value
    if bits == 1:
        return value + 1 - 2 * lax.rem(value, 2)
    if bits == 2:
        return lax.rem(value + 2, 4)
    return 3 - value


def chunk(index, size=S):
    return pl.ds(pl.multiple_of(index * size, size), size)


def dot(lhs, rhs, lhs_dim, rhs_dim):
    return lax.dot_general(lhs, rhs, (((lhs_dim,), (rhs_dim,)), ((), ())), preferred_element_type=F32)


def exchange_kernel(
    u_ref, a_hbm, b_hbm, c_hbm, d_ref, o_ref, a_out,
    fine_in, tens, cols, rets, fine_out, front, rear, diag, diag_t,
    a_ref, b_ref, c_ref, b_t, c_t, factor_sem, d_send, d_recv, *sems,
):
    row, col = lax.axis_index("row"), lax.axis_index("col")

    def row_peer(dr):
        return {"row": xor(row, dr), "col": col} if dr else None

    def col_peer(dc):
        return {"row": row, "col": xor(col, dc)} if dc else None

    def copy(src, dst, send, recv, peer):
        if not peer:
            return pltpu.make_async_copy(src, dst, recv)
        return pltpu.make_async_remote_copy(
            src_ref=src, dst_ref=dst, send_sem=send, recv_sem=recv, device_id=peer, device_id_type=MESH
        )

    def paired(which, index, offset):
        return sems[2 * which].at[index, offset], sems[2 * which + 1].at[index, offset]

    def row_round(t, dr):
        src = u_ref.at[(t + EARLY) * 4 + xor(row, dr)]
        return copy(src, tens.at[t, chunk(row)], *paired(0, t, dr), row_peer(dr))

    def row_fine(unit, dr):
        t, z = lax.div(unit, PER), lax.rem(unit, PER)
        src = u_ref.at[t * 4 + xor(row, dr), :, chunk(z, FINE), :]
        return copy(src, fine_in.at[unit, chunk(row)], *paired(1, unit, dr), row_peer(dr))

    def go_round(t, dc):
        dst = cols.at[t + EARLY, :, chunk(col), :]
        return copy(tens.at[t, chunk(xor(col, dc))], dst, *paired(2, t, dc), col_peer(dc))

    def go_fine(unit, dc):
        t, z = lax.div(unit, PER), lax.rem(unit, PER)
        dst = cols.at[t, :, chunk(col * PER + z, FINE), :]
        return copy(fine_in.at[unit, chunk(xor(col, dc))], dst, *paired(3, unit, dc), col_peer(dc))

    def back_round(t, dc):
        src = cols.at[t, :, chunk(xor(col, dc)), :]
        return copy(src, rets.at[t, chunk(col)], *paired(4, t, dc), col_peer(dc))

    def back_fine(unit, dc):
        t, z = lax.div(unit, PER) + ROUNDS - LATE, lax.rem(unit, PER)
        src = cols.at[t, :, chunk(xor(col, dc) * PER + z, FINE), :]
        return copy(src, fine_out.at[unit, chunk(col)], *paired(5, unit, dc), col_peer(dc))

    def home_round(t, dr):
        dst = o_ref.at[t * 4 + row]
        return copy(rets.at[t, chunk(xor(row, dr))], dst, *paired(6, t, dr), row_peer(dr))

    def home_fine(unit, dr):
        t, z = lax.div(unit, PER) + ROUNDS - LATE, lax.rem(unit, PER)
        dst = o_ref.at[t * 4 + row, :, chunk(z, FINE), :]
        return copy(fine_out.at[unit, chunk(xor(row, dr))], dst, *paired(7, unit, dr), row_peer(dr))

    def start(kind, index):
        for peer in (0, 3, 2, 1) if kind in (row_round, row_fine, home_round, home_fine) else (1, 2, 3, 0):
            kind(index, peer).start()

    def arrive(kind, index):
        kind(index, 0).wait()
        for peer in PEERS:
            kind(index, peer).wait_recv()

    barrier = pltpu.get_barrier_semaphore()
    for peer in PEERS:
        pl.semaphore_signal(barrier, inc=1, device_id=row_peer(peer), device_id_type=MESH)
        pl.semaphore_signal(barrier, inc=1, device_id=col_peer(peer), device_id_type=MESH)
    pl.semaphore_wait(barrier, 2 * len(PEERS))

    @pl.loop(0, PER * EARLY)
    def _(unit):
        start(row_fine, unit)

    own_d, far_d = diag.at[chunk(row, S * S)], diag.at[chunk(xor(row, 2), S * S)]
    keep_d = copy(d_ref, own_d, None, d_recv.at[0], None)
    cross_d = copy(d_ref, own_d, d_send.at[1], d_recv.at[1], row_peer(2))
    near_d = copy(d_ref, own_d, d_send.at[2], d_recv.at[2], row_peer(1))
    pass_d = copy(far_d, far_d, d_send.at[3], d_recv.at[3], row_peer(1))
    for start_d in (cross_d, near_d, keep_d):
        start_d.start()

    @pl.loop(0, 2)
    def _(t):
        start(row_round, t)

    factors = [
        pltpu.make_async_copy(a_hbm, a_ref, factor_sem.at[0]),
        pltpu.make_async_copy(b_hbm, b_ref, factor_sem.at[1]),
        pltpu.make_async_copy(c_hbm, c_ref, factor_sem.at[2]),
        pltpu.make_async_copy(a_hbm, a_out, factor_sem.at[3]),
    ]
    for factor in factors:
        factor.start()
    for factor in factors:
        factor.wait()
    b_t[...] = b_ref[...].T
    c_t[...] = c_ref[...].T

    def swapped(matrix, height):
        @pl.loop(0, height // GROUP)
        def _(step):
            lines = [pl.ds(step * GROUP + n, N, stride=height) for n in range(GROUP)]
            side = jnp.concatenate([front[line, :].astype(BF16) for line in lines], axis=1)
            both = dot(matrix[...], side, 1, 0)
            for n, line in enumerate(lines):
                rear[line, :] = both[:, n * N:(n + 1) * N]

    def first_two(view, height):
        @pl.loop(0, 4)
        def _(q):
            block = view[chunk(q)].reshape(S * height, N)
            front[chunk(q, S * height), :] = dot(block, a_ref[...], 1, 1)

        swapped(b_ref, height)

    def fifth(view, height):
        @pl.loop(0, 4)
        def _(q):
            front[chunk(q, S * height), :] = view[chunk(q)].reshape(S * height, N).astype(F32)

        swapped(b_t, height)

    def rounded(view, height):
        @pl.loop(0, 4)
        def _(q):
            view[chunk(q)] = rear[chunk(q, S * height), :].reshape(S, height, N).astype(BF16)

    def fine(here, there, buffer, work, unit):
        arrive(here, unit)
        work(buffer.at[unit], FINE)
        rounded(buffer.at[unit], FINE)
        start(there, unit)

    def whole(here, there, buffer, work, t):
        arrive(here, t)

        @pl.loop(0, S // H)
        def _(half):
            view = buffer.at[t, :, chunk(half, H), :]
            work(view, H)
            rounded(view, H)

        start(there, t)

    def middle(t, early, late):
        if early:
            for n in range(PER):
                arrive(go_fine, PER * t + n)
        else:
            arrive(go_round, t - EARLY)

        @pl.loop(0, S // GROUP)
        def _(step):
            def side(buffer):
                return jnp.concatenate([buffer[step * GROUP + n] for n in range(GROUP)], axis=1)

            h3 = (dot(c_ref[...], side(cols.at[t]), 1, 0) * side(diag_t)).astype(BF16)
            h4 = dot(c_t[...], h3, 1, 0).astype(BF16)
            for n in range(GROUP):
                cols[t, step * GROUP + n] = h4[:, n * N:(n + 1) * N]

        if late:
            for n in range(PER):
                start(back_fine, PER * (t - ROUNDS + LATE) + n)
        else:
            start(back_round, t)

    pl.loop(0, PER * EARLY)(functools.partial(fine, row_fine, go_fine, fine_in, first_two))
    cross_d.wait_recv()
    pass_d.start()
    keep_d.wait()
    near_d.wait_recv()
    pass_d.wait_recv()

    @pl.loop(0, S)
    def _(j):
        diag_t[j] = diag[pl.ds(j, N, stride=S), :].T

    def body(t, early=False, late=False, rows=False, firsts=False, fifths=True):
        middle(t, early, late)
        if rows:
            start(row_round, t + 4 - EARLY)
        if firsts:
            whole(row_round, go_round, tens, first_two, t + 2 - EARLY)
        if fifths:
            whole(back_round, home_round, rets, fifth, t - 1)

    pl.loop(0, 1)(functools.partial(body, early=True, rows=True, firsts=True, fifths=False))
    pl.loop(1, 2)(functools.partial(body, early=True, rows=True, firsts=True))
    pl.loop(2, 4)(functools.partial(body, rows=True, firsts=True))
    pl.loop(4, 6)(functools.partial(body, firsts=True))
    pl.loop(6, 7)(body)
    pl.loop(7, 8)(functools.partial(body, late=True))
    pl.loop(0, PER * LATE)(functools.partial(fine, back_fine, home_fine, fine_out, fifth))

    def finish(kinds, index):
        for kind in kinds:
            if kind in (home_round, home_fine):
                arrive(kind, index)
            for peer in PEERS:
                kind(index, peer).wait_send()

    for sent in (cross_d, near_d, pass_d):
        sent.wait_send()
    pl.loop(0, PER * EARLY)(functools.partial(finish, (row_fine, go_fine)))
    pl.loop(0, ROUNDS - EARLY)(functools.partial(finish, (row_round, go_round)))
    pl.loop(0, ROUNDS - LATE)(functools.partial(finish, (back_round, home_round)))
    pl.loop(0, PER * LATE)(functools.partial(finish, (back_fine, home_fine)))


def last_kernel(h_ref, a_ref, w_ref, out, sem):
    def store(n):
        rows = chunk(n, BLOCK)
        return pltpu.make_async_copy(out.at[rows], w_ref.at[rows], sem.at[n])

    @pl.loop(0, BLOCKS)
    def _(n):
        rows = chunk(n, BLOCK)
        out[rows, :] = dot(h_ref[rows, :], a_ref[...], 1, 0)
        store(n).start()

    @pl.loop(0, BLOCKS)
    def _(n):
        store(n).wait()


def solution(mesh):
    def local_apply(field_u, fac_a, fac_b, fac_c, diag_d):
        batch = field_u.shape[0]
        any_space = pl.BlockSpec(memory_space=pl.ANY)
        vmem = pl.BlockSpec(memory_space=pltpu.VMEM)

        def in_hbm(array):
            return pltpu.with_memory_space_constraint(array, pltpu.HBM)

        operands = (jnp.transpose(field_u, (0, 2, 3, 1)), fac_a, fac_b, fac_c, diag_d.reshape(S * S, N))
        counts = (ROUNDS - EARLY, PER * EARLY) * 2 + (ROUNDS - LATE, PER * LATE) * 2
        pairs = [pltpu.SemaphoreType.DMA((n, 4)) for n in counts for _ in range(2)]
        h5, last_a = pl.pallas_call(
            exchange_kernel,
            out_shape=(pltpu.VMEM((batch, S, S, N), BF16), pltpu.VMEM((N, N), BF16)),
            in_specs=[any_space] * 5,
            out_specs=(any_space, any_space),
            scratch_shapes=[
                pltpu.VMEM((PER * EARLY, N, FINE, N), BF16),
                pltpu.VMEM((ROUNDS - EARLY, N, S, N), BF16),
                pltpu.VMEM((ROUNDS, S, N, N), BF16),
                pltpu.VMEM((ROUNDS - LATE, N, S, N), BF16),
                pltpu.VMEM((PER * LATE, N, FINE, N), BF16),
                pltpu.VMEM((N * H, N), F32),
                pltpu.VMEM((N * H, N), F32),
                pltpu.VMEM((N * S, N), F32),
                pltpu.VMEM((S, N, N), F32),
                pltpu.VMEM((N, N), BF16),
                pltpu.VMEM((N, N), BF16),
                pltpu.VMEM((N, N), BF16),
                pltpu.VMEM((N, N), BF16),
                pltpu.VMEM((N, N), BF16),
                pltpu.SemaphoreType.DMA((4,)),
                pltpu.SemaphoreType.DMA((4,)),
                pltpu.SemaphoreType.DMA((4,)),
                *pairs,
            ],
            compiler_params=pltpu.CompilerParams(
                collective_id=0, has_side_effects=True, vmem_limit_bytes=44 * 2**20
            ),
            name="exchange",
        )(*(in_hbm(operand) for operand in operands))
        w = pl.pallas_call(
            last_kernel,
            out_shape=jax.ShapeDtypeStruct((BLOCKS * BLOCK, N), F32),
            in_specs=[vmem, vmem],
            out_specs=any_space,
            scratch_shapes=[pltpu.VMEM((BLOCKS * BLOCK, N), F32), pltpu.SemaphoreType.DMA((BLOCKS,))],
            compiler_params=pltpu.CompilerParams(vmem_limit_bytes=24 * 2**20),
            name="last",
        )(h5.reshape(BLOCKS * BLOCK, N), last_a)
        return jnp.transpose(w.reshape(batch, S, S, N), (0, 3, 1, 2))

    spec_field = P("fields", None, "row", "col")
    spec_factor = P("fields", None)
    return jax.shard_map(
        local_apply,
        mesh=mesh,
        in_specs=(spec_field, spec_factor, spec_factor, spec_factor, P(("fields", "row"), "col", None)),
        out_specs=spec_field,
        check_vma=False,
    )
```

time: 397 us -> 397 us (level)
  no operation moved by 1% of the time
where the time goes in v6:
time: 397 us; the launch traced here: 394 us
  Pallas kernels  394 us (99%)
    pallas_call x1, Pallas kernels, local_apply(): pl.pallas_call(exchange_kernel, out_shape=(pltpu.VMEM((batch, S, S, N), B...  387 us

profile of v6, /device:TPU:0, one launch (start us, length us, event | category | flops | bytes accessed | tf_op | source)
XLA Modules:
  0.0 393.8 jit_solution(10900811584723321184)
XLA Ops:
  0.0 387.5 %exchange.1 = (bf16[32,32,32,128]{3,2,1,0:T(8,128)(2,1)S(1)}, bf16[128,128]{1,0:T(8,128)(2,1)S(1)}) custom-call(bf16[32,32,32,128]{3,2,1,0:T(8,128)(2,1)} %bitcast.7, bf16[128,128]{1,0:T(8,128)(2,1)} %a_hbm.1, bf16[128,128]{1,0:T(8,128)(2,1)} %b_hbm.1, bf16[128,128]{1,0:T(8,128)(2,1)} %c_hbm.1, f32[1024,128]{1,0:T(8,128)} %bitcast.8), custom_call_target="tpu_custom_call" | custom-call | tf_op jit(solution)/shard_map/exchange/pallas_call | solution.py:286
  387.5 6.3 %last.1 = f32[32768,128]{1,0:T(8,128)} custom-call(bf16[32768,128]{1,0:T(8,128)(2,1)S(1)} %bitcast.6, bf16[128,128]{1,0:T(8,128)(2,1)S(1)} %get-tuple-element.8.a_ref), custom_call_target="tpu_custom_call" | custom-call | tf_op jit(solution)/shard_map/last/pallas_call | solution.py:316

commit v7 on v6

--- a/solution.py
+++ b/solution.py
@@ -16,6 +16,7 @@
 ROUNDS = 8
 EARLY = 2
 LATE = 1
+LEAD = 4
 GROUP = 4
 BLOCKS, BLOCK = 8, 4096
 F32, BF16 = jnp.float32, jnp.bfloat16
@@ -126,7 +127,7 @@
     for start_d in (cross_d, near_d, keep_d):
         start_d.start()
 
-    @pl.loop(0, 2)
+    @pl.loop(0, ROUNDS - EARLY)
     def _(t):
         start(row_round, t)
 
@@ -223,21 +224,22 @@
     def _(j):
         diag_t[j] = diag[pl.ds(j, N, stride=S), :].T
 
-    def body(t, early=False, late=False, rows=False, firsts=False, fifths=True):
+    first_round = functools.partial(whole, row_round, go_round, tens, first_two)
+    fifth_round = functools.partial(whole, back_round, home_round, rets, fifth)
+
+    def body(t, early=False, late=False, firsts=False, fifths=True):
         middle(t, early, late)
-        if rows:
-            start(row_round, t + 4 - EARLY)
         if firsts:
-            whole(row_round, go_round, tens, first_two, t + 2 - EARLY)
+            first_round(t + LEAD - EARLY)
         if fifths:
-            whole(back_round, home_round, rets, fifth, t - 1)
-
-    pl.loop(0, 1)(functools.partial(body, early=True, rows=True, firsts=True, fifths=False))
-    pl.loop(1, 2)(functools.partial(body, early=True, rows=True, firsts=True))
-    pl.loop(2, 4)(functools.partial(body, rows=True, firsts=True))
-    pl.loop(4, 6)(functools.partial(body, firsts=True))
-    pl.loop(6, 7)(body)
+            fifth_round(t - 2)
+
+    pl.loop(0, LEAD - EARLY)(first_round)
+    pl.loop(0, 2)(functools.partial(body, early=True, firsts=True, fifths=False))
+    pl.loop(2, 4)(functools.partial(body, firsts=True))
+    pl.loop(4, 7)(body)
     pl.loop(7, 8)(functools.partial(body, late=True))
+    pl.loop(6, 7)(fifth_round)
     pl.loop(0, PER * LATE)(functools.partial(fine, back_fine, home_fine, fine_out, fifth))
 
     def finish(kinds, index):

time: 397 us -> 396 us (level)
  no operation moved by 1% of the time
where the time goes in v7:
time: 396 us; the launch traced here: 392 us
  Pallas kernels  392 us (99%)
    pallas_call x1, Pallas kernels, local_apply(): pl.pallas_call(exchange_kernel, out_shape=(pltpu.VMEM((batch, S, S, N), B...  386 us

profile of v7, /device:TPU:0, one launch (start us, length us, event | category | flops | bytes accessed | tf_op | source)
XLA Modules:
  0.0 392.4 jit_solution(12610687423402874986)
XLA Ops:
  0.0 386.1 %exchange.1 = (bf16[32,32,32,128]{3,2,1,0:T(8,128)(2,1)S(1)}, bf16[128,128]{1,0:T(8,128)(2,1)S(1)}) custom-call(bf16[32,32,32,128]{3,2,1,0:T(8,128)(2,1)} %bitcast.7, bf16[128,128]{1,0:T(8,128)(2,1)} %a_hbm.1, bf16[128,128]{1,0:T(8,128)(2,1)} %b_hbm.1, bf16[128,128]{1,0:T(8,128)(2,1)} %c_hbm.1, f32[1024,128]{1,0:T(8,128)} %bitcast.8), custom_call_target="tpu_custom_call" | custom-call | tf_op jit(solution)/shard_map/exchange/pallas_call | solution.py:288
  386.1 6.3 %last.1 = f32[32768,128]{1,0:T(8,128)} custom-call(bf16[32768,128]{1,0:T(8,128)(2,1)S(1)} %bitcast.6, bf16[128,128]{1,0:T(8,128)(2,1)S(1)} %get-tuple-element.8.a_ref), custom_call_target="tpu_custom_call" | custom-call | tf_op jit(solution)/shard_map/last/pallas_call | solution.py:318

commit v8 on v7

--- a/solution.py
+++ b/solution.py
@@ -14,11 +14,11 @@
 FINE = 8
 PER = S // FINE
 ROUNDS = 8
-EARLY = 2
+EARLY = 1
 LATE = 1
 LEAD = 4
 GROUP = 4
-BLOCKS, BLOCK = 8, 4096
+BLOCKS, BLOCK = 16, 2048
 F32, BF16 = jnp.float32, jnp.bfloat16
 PEERS = (1, 2, 3)
 
@@ -74,21 +74,21 @@
         return copy(src, fine_in.at[unit, chunk(row)], *paired(1, unit, dr), row_peer(dr))
 
     def go_round(t, dc):
-        dst = cols.at[t + EARLY, :, chunk(col), :]
+        dst = cols.at[t + EARLY, col]
         return copy(tens.at[t, chunk(xor(col, dc))], dst, *paired(2, t, dc), col_peer(dc))
 
     def go_fine(unit, dc):
         t, z = lax.div(unit, PER), lax.rem(unit, PER)
-        dst = cols.at[t, :, chunk(col * PER + z, FINE), :]
+        dst = cols.at[t, col, :, chunk(z, FINE), :]
         return copy(fine_in.at[unit, chunk(xor(col, dc))], dst, *paired(3, unit, dc), col_peer(dc))
 
     def back_round(t, dc):
-        src = cols.at[t, :, chunk(xor(col, dc)), :]
+        src = cols.at[t, xor(col, dc)]
         return copy(src, rets.at[t, chunk(col)], *paired(4, t, dc), col_peer(dc))
 
     def back_fine(unit, dc):
         t, z = lax.div(unit, PER) + ROUNDS - LATE, lax.rem(unit, PER)
-        src = cols.at[t, :, chunk(xor(col, dc) * PER + z, FINE), :]
+        src = cols.at[t, xor(col, dc), :, chunk(z, FINE), :]
         return copy(src, fine_out.at[unit, chunk(col)], *paired(5, unit, dc), col_peer(dc))
 
     def home_round(t, dr):
@@ -118,6 +118,8 @@
     @pl.loop(0, PER * EARLY)
     def _(unit):
         start(row_fine, unit)
+
+    start(row_round, 0)
 
     own_d, far_d = diag.at[chunk(row, S * S)], diag.at[chunk(xor(row, 2), S * S)]
     keep_d = copy(d_ref, own_d, None, d_recv.at[0], None)
@@ -127,7 +129,7 @@
     for start_d in (cross_d, near_d, keep_d):
         start_d.start()
 
-    @pl.loop(0, ROUNDS - EARLY)
+    @pl.loop(1, ROUNDS - EARLY)
     def _(t):
         start(row_round, t)
 
@@ -199,13 +201,17 @@
 
         @pl.loop(0, S // GROUP)
         def _(step):
-            def side(buffer):
-                return jnp.concatenate([buffer[step * GROUP + n] for n in range(GROUP)], axis=1)
-
-            h3 = (dot(c_ref[...], side(cols.at[t]), 1, 0) * side(diag_t)).astype(BF16)
+            def slab(j):
+                return jnp.concatenate([cols[t, c, j] for c in range(4)], axis=0)
+
+            js = [step * GROUP + n for n in range(GROUP)]
+            h2 = jnp.concatenate([slab(j) for j in js], axis=1)
+            scale = jnp.concatenate([diag_t[j] for j in js], axis=1)
+            h3 = (dot(c_ref[...], h2, 1, 0) * scale).astype(BF16)
             h4 = dot(c_t[...], h3, 1, 0).astype(BF16)
-            for n in range(GROUP):
-                cols[t, step * GROUP + n] = h4[:, n * N:(n + 1) * N]
+            for n, j in enumerate(js):
+                for c in range(4):
+                    cols[t, c, j] = h4[c * S:(c + 1) * S, n * N:(n + 1) * N]
 
         if late:
             for n in range(PER):
@@ -213,7 +219,11 @@
         else:
             start(back_round, t)
 
+    first_round = functools.partial(whole, row_round, go_round, tens, first_two)
+    fifth_round = functools.partial(whole, back_round, home_round, rets, fifth)
+
     pl.loop(0, PER * EARLY)(functools.partial(fine, row_fine, go_fine, fine_in, first_two))
+    pl.loop(0, 1)(first_round)
     cross_d.wait_recv()
     pass_d.start()
     keep_d.wait()
@@ -223,9 +233,6 @@
     @pl.loop(0, S)
     def _(j):
         diag_t[j] = diag[pl.ds(j, N, stride=S), :].T
-
-    first_round = functools.partial(whole, row_round, go_round, tens, first_two)
-    fifth_round = functools.partial(whole, back_round, home_round, rets, fifth)
 
     def body(t, early=False, late=False, firsts=False, fifths=True):
         middle(t, early, late)
@@ -234,8 +241,9 @@
         if fifths:
             fifth_round(t - 2)
 
-    pl.loop(0, LEAD - EARLY)(first_round)
-    pl.loop(0, 2)(functools.partial(body, early=True, firsts=True, fifths=False))
+    pl.loop(1, LEAD - EARLY)(first_round)
+    pl.loop(0, 1)(functools.partial(body, early=True, firsts=True, fifths=False))
+    pl.loop(1, 2)(functools.partial(body, firsts=True, fifths=False))
     pl.loop(2, 4)(functools.partial(body, firsts=True))
     pl.loop(4, 7)(body)
     pl.loop(7, 8)(functools.partial(body, late=True))
@@ -293,7 +301,7 @@
             scratch_shapes=[
                 pltpu.VMEM((PER * EARLY, N, FINE, N), BF16),
                 pltpu.VMEM((ROUNDS - EARLY, N, S, N), BF16),
-                pltpu.VMEM((ROUNDS, S, N, N), BF16),
+                pltpu.VMEM((ROUNDS, 4, S, S, N), BF16),
                 pltpu.VMEM((ROUNDS - LATE, N, S, N), BF16),
                 pltpu.VMEM((PER * LATE, N, FINE, N), BF16),
                 pltpu.VMEM((N * H, N), F32),

time: 396 us -> 395 us (level)
  no operation moved by 1% of the time
where the time goes in v8:
time: 395 us; the launch traced here: 392 us
  Pallas kernels  392 us (99%)
    pallas_call x1, Pallas kernels, local_apply(): pl.pallas_call(exchange_kernel, out_shape=(pltpu.VMEM((batch, S, S, N), B...  386 us

profile of v8, /device:TPU:0, one launch (start us, length us, event | category | flops | bytes accessed | tf_op | source)
XLA Modules:
  0.0 392.1 jit_solution(5302412418486618432)
XLA Ops:
  0.0 385.9 %exchange.1 = (bf16[32,32,32,128]{3,2,1,0:T(8,128)(2,1)S(1)}, bf16[128,128]{1,0:T(8,128)(2,1)S(1)}) custom-call(bf16[32,32,32,128]{3,2,1,0:T(8,128)(2,1)} %bitcast.7, bf16[128,128]{1,0:T(8,128)(2,1)} %a_hbm.1, bf16[128,128]{1,0:T(8,128)(2,1)} %b_hbm.1, bf16[128,128]{1,0:T(8,128)(2,1)} %c_hbm.1, f32[1024,128]{1,0:T(8,128)} %bitcast.8), custom_call_target="tpu_custom_call" | custom-call | tf_op jit(solution)/shard_map/exchange/pallas_call | solution.py:296
  385.9 6.2 %last.1 = f32[32768,128]{1,0:T(8,128)} custom-call(bf16[32768,128]{1,0:T(8,128)(2,1)S(1)} %bitcast.6, bf16[128,128]{1,0:T(8,128)(2,1)S(1)} %get-tuple-element.8.a_ref), custom_call_target="tpu_custom_call" | custom-call | tf_op jit(solution)/shard_map/last/pallas_call | solution.py:326

commit v9 on v8

--- a/solution.py
+++ b/solution.py
@@ -16,7 +16,6 @@
 ROUNDS = 8
 EARLY = 1
 LATE = 1
-LEAD = 4
 GROUP = 4
 BLOCKS, BLOCK = 16, 2048
 F32, BF16 = jnp.float32, jnp.bfloat16
@@ -234,20 +233,11 @@
     def _(j):
         diag_t[j] = diag[pl.ds(j, N, stride=S), :].T
 
-    def body(t, early=False, late=False, firsts=False, fifths=True):
-        middle(t, early, late)
-        if firsts:
-            first_round(t + LEAD - EARLY)
-        if fifths:
-            fifth_round(t - 2)
-
-    pl.loop(1, LEAD - EARLY)(first_round)
-    pl.loop(0, 1)(functools.partial(body, early=True, firsts=True, fifths=False))
-    pl.loop(1, 2)(functools.partial(body, firsts=True, fifths=False))
-    pl.loop(2, 4)(functools.partial(body, firsts=True))
-    pl.loop(4, 7)(body)
-    pl.loop(7, 8)(functools.partial(body, late=True))
-    pl.loop(6, 7)(fifth_round)
+    pl.loop(1, ROUNDS - EARLY)(first_round)
+    pl.loop(0, EARLY)(functools.partial(middle, early=True, late=False))
+    pl.loop(EARLY, ROUNDS - LATE)(functools.partial(middle, early=False, late=False))
+    pl.loop(ROUNDS - LATE, ROUNDS)(functools.partial(middle, early=False, late=True))
+    pl.loop(0, ROUNDS - LATE)(fifth_round)
     pl.loop(0, PER * LATE)(functools.partial(fine, back_fine, home_fine, fine_out, fifth))
 
     def finish(kinds, index):

time: 395 us -> 395 us (level)
  no operation moved by 1% of the time
where the time goes in v9:
time: 395 us; the launch traced here: 391 us
  Pallas kernels  391 us (99%)
    pallas_call x1, Pallas kernels, local_apply(): pl.pallas_call(exchange_kernel, out_shape=(pltpu.VMEM((batch, S, S, N), B...  385 us

profile of v9, /device:TPU:0, one launch (start us, length us, event | category | flops | bytes accessed | tf_op | source)
XLA Modules:
  0.0 391.5 jit_solution(8496844264621784776)
XLA Ops:
  0.0 385.2 %exchange.1 = (bf16[32,32,32,128]{3,2,1,0:T(8,128)(2,1)S(1)}, bf16[128,128]{1,0:T(8,128)(2,1)S(1)}) custom-call(bf16[32,32,32,128]{3,2,1,0:T(8,128)(2,1)} %bitcast.7, bf16[128,128]{1,0:T(8,128)(2,1)} %a_hbm.1, bf16[128,128]{1,0:T(8,128)(2,1)} %b_hbm.1, bf16[128,128]{1,0:T(8,128)(2,1)} %c_hbm.1, f32[1024,128]{1,0:T(8,128)} %bitcast.8), custom_call_target="tpu_custom_call" | custom-call | tf_op jit(solution)/shard_map/exchange/pallas_call | solution.py:286
  385.2 6.2 %last.1 = f32[32768,128]{1,0:T(8,128)} custom-call(bf16[32768,128]{1,0:T(8,128)(2,1)S(1)} %bitcast.6, bf16[128,128]{1,0:T(8,128)(2,1)S(1)} %get-tuple-element.8.a_ref), custom_call_target="tpu_custom_call" | custom-call | tf_op jit(solution)/shard_map/last/pallas_call | solution.py:316

commit v10 on v9

--- a/solution.py
+++ b/solution.py
@@ -181,7 +181,8 @@
         start(there, unit)
 
     def whole(here, there, buffer, work, t):
-        arrive(here, t)
+        if here:
+            arrive(here, t)
 
         @pl.loop(0, S // H)
         def _(half):
@@ -191,7 +192,7 @@
 
         start(there, t)
 
-    def middle(t, early, late):
+    def middle(t, early):
         if early:
             for n in range(PER):
                 arrive(go_fine, PER * t + n)
@@ -212,6 +213,7 @@
                 for c in range(4):
                     cols[t, c, j] = h4[c * S:(c + 1) * S, n * N:(n + 1) * N]
 
+    def send_back(t, late):
         if late:
             for n in range(PER):
                 start(back_fine, PER * (t - ROUNDS + LATE) + n)
@@ -219,7 +221,7 @@
             start(back_round, t)
 
     first_round = functools.partial(whole, row_round, go_round, tens, first_two)
-    fifth_round = functools.partial(whole, back_round, home_round, rets, fifth)
+    fifth_round = functools.partial(whole, None, home_round, rets, fifth)
 
     pl.loop(0, PER * EARLY)(functools.partial(fine, row_fine, go_fine, fine_in, first_two))
     pl.loop(0, 1)(first_round)
@@ -234,10 +236,29 @@
         diag_t[j] = diag[pl.ds(j, N, stride=S), :].T
 
     pl.loop(1, ROUNDS - EARLY)(first_round)
-    pl.loop(0, EARLY)(functools.partial(middle, early=True, late=False))
-    pl.loop(EARLY, ROUNDS - LATE)(functools.partial(middle, early=False, late=False))
-    pl.loop(ROUNDS - LATE, ROUNDS)(functools.partial(middle, early=False, late=True))
-    pl.loop(0, ROUNDS - LATE)(fifth_round)
+    at_end = lax.rem(col, 3) == 0
+
+    def body(t, early=False, late=False, fifths=True):
+        middle(t, early)
+        if not fifths:
+            send_back(t, late)
+            return
+
+        @pl.when(jnp.logical_not(at_end))
+        def _():
+            send_back(t, late)
+
+        arrive(back_round, t - 1)
+
+        @pl.when(at_end)
+        def _():
+            send_back(t, late)
+
+        fifth_round(t - 1)
+
+    pl.loop(0, 1)(functools.partial(body, early=True, fifths=False))
+    pl.loop(1, ROUNDS - LATE)(body)
+    pl.loop(ROUNDS - LATE, ROUNDS)(functools.partial(body, late=True))
     pl.loop(0, PER * LATE)(functools.partial(fine, back_fine, home_fine, fine_out, fifth))
 
     def finish(kinds, index):

time: 395 us -> 390 us (0.987)
  Pallas kernels: 391 us -> 387 us
    pallas_call x1, Pallas kernels: 385 us -> 381 us  [local_apply(): pl.pallas_call(exchange_kernel, out_shape=(pltpu.VMEM((batch, S, S, N), B...]
where the time goes in v10:
time: 390 us; the launch traced here: 387 us
  Pallas kernels  387 us (99%)
    pallas_call x1, Pallas kernels, local_apply(): pl.pallas_call(exchange_kernel, out_shape=(pltpu.VMEM((batch, S, S, N), B...  381 us

profile of v10, /device:TPU:0, one launch (start us, length us, event | category | flops | bytes accessed | tf_op | source)
XLA Modules:
  0.0 387.2 jit_solution(4868414061011915584)
XLA Ops:
  0.0 380.9 %exchange.1 = (bf16[32,32,32,128]{3,2,1,0:T(8,128)(2,1)S(1)}, bf16[128,128]{1,0:T(8,128)(2,1)S(1)}) custom-call(bf16[32,32,32,128]{3,2,1,0:T(8,128)(2,1)} %bitcast.7, bf16[128,128]{1,0:T(8,128)(2,1)} %a_hbm.1, bf16[128,128]{1,0:T(8,128)(2,1)} %b_hbm.1, bf16[128,128]{1,0:T(8,128)(2,1)} %c_hbm.1, f32[1024,128]{1,0:T(8,128)} %bitcast.8), custom_call_target="tpu_custom_call" | custom-call | tf_op jit(solution)/shard_map/exchange/pallas_call | solution.py:307
  380.9 6.2 %last.1 = f32[32768,128]{1,0:T(8,128)} custom-call(bf16[32768,128]{1,0:T(8,128)(2,1)S(1)} %bitcast.6, bf16[128,128]{1,0:T(8,128)(2,1)S(1)} %get-tuple-element.8.a_ref), custom_call_target="tpu_custom_call" | custom-call | tf_op jit(solution)/shard_map/last/pallas_call | solution.py:337

commit v11 on v10

--- a/solution.py
+++ b/solution.py
@@ -100,7 +100,7 @@
         return copy(fine_out.at[unit, chunk(xor(row, dr))], dst, *paired(7, unit, dr), row_peer(dr))
 
     def start(kind, index):
-        for peer in (0, 3, 2, 1) if kind in (row_round, row_fine, home_round, home_fine) else (1, 2, 3, 0):
+        for peer in (3, 2, 1, 0) if kind in (row_round, row_fine, home_round, home_fine) else (1, 2, 3, 0):
             kind(index, peer).start()
 
     def arrive(kind, index):
@@ -114,7 +114,14 @@
         pl.semaphore_signal(barrier, inc=1, device_id=col_peer(peer), device_id_type=MESH)
     pl.semaphore_wait(barrier, 2 * len(PEERS))
 
-    @pl.loop(0, PER * EARLY)
+    for core, order in enumerate(((2, 3, 1, 0), (3, 2, 1, 0))):
+
+        @pl.when(lax.rem(row, 2) == core)
+        def _():
+            for peer in order:
+                row_fine(0, peer).start()
+
+    @pl.loop(1, PER * EARLY)
     def _(unit):
         start(row_fine, unit)
 

time: 390 us -> 391 us (level)
  no operation moved by 1% of the time
where the time goes in v11:
time: 391 us; the launch traced here: 388 us
  Pallas kernels  388 us (99%)
    pallas_call x1, Pallas kernels, local_apply(): pl.pallas_call(exchange_kernel, out_shape=(pltpu.VMEM((batch, S, S, N), B...  382 us

profile of v11, /device:TPU:0, one launch (start us, length us, event | category | flops | bytes accessed | tf_op | source)
XLA Modules:
  0.0 388.4 jit_solution(17795241909623648937)
XLA Ops:
  0.0 382.2 %exchange.1 = (bf16[32,32,32,128]{3,2,1,0:T(8,128)(2,1)S(1)}, bf16[128,128]{1,0:T(8,128)(2,1)S(1)}) custom-call(bf16[32,32,32,128]{3,2,1,0:T(8,128)(2,1)} %bitcast.7, bf16[128,128]{1,0:T(8,128)(2,1)} %a_hbm.1, bf16[128,128]{1,0:T(8,128)(2,1)} %b_hbm.1, bf16[128,128]{1,0:T(8,128)(2,1)} %c_hbm.1, f32[1024,128]{1,0:T(8,128)} %bitcast.8), custom_call_target="tpu_custom_call" | custom-call | tf_op jit(solution)/shard_map/exchange/pallas_call | solution.py:314
  382.2 6.2 %last.1 = f32[32768,128]{1,0:T(8,128)} custom-call(bf16[32768,128]{1,0:T(8,128)(2,1)S(1)} %bitcast.6, bf16[128,128]{1,0:T(8,128)(2,1)S(1)} %get-tuple-element.8.a_ref), custom_call_target="tpu_custom_call" | custom-call | tf_op jit(solution)/shard_map/last/pallas_call | solution.py:344

commit v12 on v10

--- a/solution.py
+++ b/solution.py
@@ -100,7 +100,7 @@
         return copy(fine_out.at[unit, chunk(xor(row, dr))], dst, *paired(7, unit, dr), row_peer(dr))
 
     def start(kind, index):
-        for peer in (0, 3, 2, 1) if kind in (row_round, row_fine, home_round, home_fine) else (1, 2, 3, 0):
+        for peer in (0, 3, 2, 1) if kind in (row_round, row_fine, home_round, home_fine) else (3, 2, 1, 0):
             kind(index, peer).start()
 
     def arrive(kind, index):

time: 390 us -> 385 us (0.987)
  no operation moved by 1% of the time
where the time goes in v12:
time: 385 us
  Pallas kernels  385 us (100%)
    pallas_call x1, Pallas kernels, local_apply(): pl.pallas_call(exchange_kernel, out_shape=(pltpu.VMEM((batch, S, S, N), B...  378 us

profile of v12, /device:TPU:0, one launch (start us, length us, event | category | flops | bytes accessed | tf_op | source)
XLA Modules:
  0.0 384.6 jit_solution(5185733088600048910)
XLA Ops:
  0.0 378.4 %exchange.1 = (bf16[32,32,32,128]{3,2,1,0:T(8,128)(2,1)S(1)}, bf16[128,128]{1,0:T(8,128)(2,1)S(1)}) custom-call(bf16[32,32,32,128]{3,2,1,0:T(8,128)(2,1)} %bitcast.7, bf16[128,128]{1,0:T(8,128)(2,1)} %a_hbm.1, bf16[128,128]{1,0:T(8,128)(2,1)} %b_hbm.1, bf16[128,128]{1,0:T(8,128)(2,1)} %c_hbm.1, f32[1024,128]{1,0:T(8,128)} %bitcast.8), custom_call_target="tpu_custom_call" | custom-call | tf_op jit(solution)/shard_map/exchange/pallas_call | solution.py:307
  378.4 6.2 %last.1 = f32[32768,128]{1,0:T(8,128)} custom-call(bf16[32768,128]{1,0:T(8,128)(2,1)S(1)} %bitcast.6, bf16[128,128]{1,0:T(8,128)(2,1)S(1)} %get-tuple-element.8.a_ref), custom_call_target="tpu_custom_call" | custom-call | tf_op jit(solution)/shard_map/last/pallas_call | solution.py:337

commit v13 on v12

--- a/solution.py
+++ b/solution.py
@@ -100,7 +100,7 @@
         return copy(fine_out.at[unit, chunk(xor(row, dr))], dst, *paired(7, unit, dr), row_peer(dr))
 
     def start(kind, index):
-        for peer in (0, 3, 2, 1) if kind in (row_round, row_fine, home_round, home_fine) else (3, 2, 1, 0):
+        for peer in (0, 3, 2, 1) if kind in (row_round, row_fine, home_round, home_fine) else (2, 3, 1, 0):
             kind(index, peer).start()
 
     def arrive(kind, index):

time: 385 us -> 393 us (1.021)
  the two profiles are of different devices: /device:TPU:0 before, /device:TPU:14 now
where the time goes in v13:
time: 393 us
  Pallas kernels  393 us (100%)
    pallas_call x1, Pallas kernels, local_apply(): pl.pallas_call(exchange_kernel, out_shape=(pltpu.VMEM((batch, S, S, N), B...  387 us

profile of v13, /device:TPU:14, one launch (start us, length us, event | category | flops | bytes accessed | tf_op | source)
XLA Modules:
  0.0 392.8 jit_solution(4355029953184465925)
XLA Ops:
  0.0 386.5 %exchange.1 = (bf16[32,32,32,128]{3,2,1,0:T(8,128)(2,1)S(1)}, bf16[128,128]{1,0:T(8,128)(2,1)S(1)}) custom-call(bf16[32,32,32,128]{3,2,1,0:T(8,128)(2,1)} %bitcast.7, bf16[128,128]{1,0:T(8,128)(2,1)} %a_hbm.1, bf16[128,128]{1,0:T(8,128)(2,1)} %b_hbm.1, bf16[128,128]{1,0:T(8,128)(2,1)} %c_hbm.1, f32[1024,128]{1,0:T(8,128)} %bitcast.8), custom_call_target="tpu_custom_call" | custom-call | tf_op jit(solution)/shard_map/exchange/pallas_call | solution.py:307
  386.5 6.2 %last.1 = f32[32768,128]{1,0:T(8,128)} custom-call(bf16[32768,128]{1,0:T(8,128)(2,1)S(1)} %bitcast.6, bf16[128,128]{1,0:T(8,128)(2,1)S(1)} %get-tuple-element.8.a_ref), custom_call_target="tpu_custom_call" | custom-call | tf_op jit(solution)/shard_map/last/pallas_call | solution.py:337

commit v14 on v11

--- a/solution.py
+++ b/solution.py
@@ -100,7 +100,7 @@
         return copy(fine_out.at[unit, chunk(xor(row, dr))], dst, *paired(7, unit, dr), row_peer(dr))
 
     def start(kind, index):
-        for peer in (3, 2, 1, 0) if kind in (row_round, row_fine, home_round, home_fine) else (1, 2, 3, 0):
+        for peer in (0, 3, 2, 1) if kind in (row_round, row_fine, home_round, home_fine) else (3, 2, 1, 0):
             kind(index, peer).start()
 
     def arrive(kind, index):

time: 391 us -> 385 us (0.985)
  no operation moved by 1% of the time
where the time goes in v14:
time: 385 us
  Pallas kernels  385 us (100%)
    pallas_call x1, Pallas kernels, local_apply(): pl.pallas_call(exchange_kernel, out_shape=(pltpu.VMEM((batch, S, S, N), B...  379 us

profile of v14, /device:TPU:0, one launch (start us, length us, event | category | flops | bytes accessed | tf_op | source)
XLA Modules:
  0.0 385.3 jit_solution(7701623486966163970)
XLA Ops:
  0.0 379.1 %exchange.1 = (bf16[32,32,32,128]{3,2,1,0:T(8,128)(2,1)S(1)}, bf16[128,128]{1,0:T(8,128)(2,1)S(1)}) custom-call(bf16[32,32,32,128]{3,2,1,0:T(8,128)(2,1)} %bitcast.7, bf16[128,128]{1,0:T(8,128)(2,1)} %a_hbm.1, bf16[128,128]{1,0:T(8,128)(2,1)} %b_hbm.1, bf16[128,128]{1,0:T(8,128)(2,1)} %c_hbm.1, f32[1024,128]{1,0:T(8,128)} %bitcast.8), custom_call_target="tpu_custom_call" | custom-call | tf_op jit(solution)/shard_map/exchange/pallas_call | solution.py:314
  379.1 6.2 %last.1 = f32[32768,128]{1,0:T(8,128)} custom-call(bf16[32768,128]{1,0:T(8,128)(2,1)S(1)} %bitcast.6, bf16[128,128]{1,0:T(8,128)(2,1)S(1)} %get-tuple-element.8.a_ref), custom_call_target="tpu_custom_call" | custom-call | tf_op jit(solution)/shard_map/last/pallas_call | solution.py:344

commit v15 on v12

--- a/solution.py
+++ b/solution.py
@@ -99,6 +99,16 @@
         dst = o_ref.at[t * 4 + row, :, chunk(z, FINE), :]
         return copy(fine_out.at[unit, chunk(xor(row, dr))], dst, *paired(7, unit, dr), row_peer(dr))
 
+    at_end = lax.rem(col, 3) == 0
+
+    def start_back_fine(unit):
+        for here, order in ((at_end, (3, 2, 1, 0)), (jnp.logical_not(at_end), (1, 3, 2, 0))):
+
+            @pl.when(here)
+            def _():
+                for peer in order:
+                    back_fine(unit, peer).start()
+
     def start(kind, index):
         for peer in (0, 3, 2, 1) if kind in (row_round, row_fine, home_round, home_fine) else (3, 2, 1, 0):
             kind(index, peer).start()
@@ -216,7 +226,7 @@
     def send_back(t, late):
         if late:
             for n in range(PER):
-                start(back_fine, PER * (t - ROUNDS + LATE) + n)
+                start_back_fine(PER * (t - ROUNDS + LATE) + n)
         else:
             start(back_round, t)
 
@@ -236,8 +246,6 @@
         diag_t[j] = diag[pl.ds(j, N, stride=S), :].T
 
     pl.loop(1, ROUNDS - EARLY)(first_round)
-    at_end = lax.rem(col, 3) == 0
-
     def body(t, early=False, late=False, fifths=True):
         middle(t, early)
         if not fifths:

time: 385 us -> 385 us (level)
  no operation moved by 1% of the time
where the time goes in v15:
time: 385 us
  Pallas kernels  385 us (100%)
    pallas_call x1, Pallas kernels, local_apply(): pl.pallas_call(exchange_kernel, out_shape=(pltpu.VMEM((batch, S, S, N), B...  378 us

profile of v15, /device:TPU:0, one launch (start us, length us, event | category | flops | bytes accessed | tf_op | source)
XLA Modules:
  0.0 384.6 jit_solution(14712053812711643565)
XLA Ops:
  0.0 378.4 %exchange.1 = (bf16[32,32,32,128]{3,2,1,0:T(8,128)(2,1)S(1)}, bf16[128,128]{1,0:T(8,128)(2,1)S(1)}) custom-call(bf16[32,32,32,128]{3,2,1,0:T(8,128)(2,1)} %bitcast.7, bf16[128,128]{1,0:T(8,128)(2,1)} %a_hbm.1, bf16[128,128]{1,0:T(8,128)(2,1)} %b_hbm.1, bf16[128,128]{1,0:T(8,128)(2,1)} %c_hbm.1, f32[1024,128]{1,0:T(8,128)} %bitcast.8), custom_call_target="tpu_custom_call" | custom-call | tf_op jit(solution)/shard_map/exchange/pallas_call | solution.py:315
  378.4 6.2 %last.1 = f32[32768,128]{1,0:T(8,128)} custom-call(bf16[32768,128]{1,0:T(8,128)(2,1)S(1)} %bitcast.6, bf16[128,128]{1,0:T(8,128)(2,1)S(1)} %get-tuple-element.8.a_ref), custom_call_target="tpu_custom_call" | custom-call | tf_op jit(solution)/shard_map/last/pallas_call | solution.py:345
